TPU v7x, 32 devices: a whole 2x2x4 slice. The times are simulated.
32 devices in a mesh: tm: 16 (over z, x, core), gz: 2 (over y).
Axes of the slice: x: 2, y: 2, z: 4, core: 2. Of those that a mesh axis runs over, the one named last changes fastest.
Arguments:
- starts: float32 [16, 8, 32, 128], P('tm', 'gz'), may hold values from -6 to 6
- cell_rates: float32 [8, 32, 128], P('gz'), may hold values from 0.3 to 1
Outputs:
- slab_ends: float32 [16, 8, 32, 128], P('tm', 'gz')
- next_starts: float32 [16, 8, 32, 128], P('tm', 'gz')
All inputs are finite; a program needn't handle non-finite values.
Results may differ from a plain program's by a relative error of at most 0.0001.
Values sent between devices are 32-bit elements; how exact they have to be, the bound alone decides.
A program may use at most 64 MiB of HBM per device.

v0:
```python
import functools

import jax
import jax.numpy as jnp
from jax import lax
from jax.experimental import pallas as pl
from jax.experimental.pallas import tpu as pltpu
from jax.sharding import PartitionSpec as P

MESH = pl.DeviceIdType.MESH
FINE = 4

fine_along_z = (0.1, 0.12)
fine_along_x = (0.15, 0.12)
fine_along_y = (0.2, 0.12)
coarse_along_z = (0.2, 0.25)
coarse_along_x = (0.3, 0.25)
coarse_along_y = (0.4, 0.25)


def line_filter(behind, middle, beyond, along):
    courant, diffuse = along
    return (
        (diffuse + 0.5 * courant) * behind
        + (1.0 - 2.0 * diffuse) * middle
        + (diffuse - 0.5 * courant) * beyond
    )


def turned(values, by, dim):
    return pltpu.roll(values, by % values.shape[dim], dim)


def filtered(values, by, dim, along):
    return line_filter(turned(values, by, dim), values, turned(values, -by, dim), along)


def row_size(slabs):
    return next(q for q in range(1, slabs + 1) if slabs % q == 0 and q * q >= slabs)


def group_size(slabs):
    return 2 if slabs % 2 == 0 else 1


def rounds(lines):
    reaches, known = [], 1
    while known < lines:
        reaches.append(known)
        known *= 2
    return reaches


def pair_size(size, depth):
    return 2 if size % 2 == 0 and depth % 2 == 0 else 1


def kernel(
    slabs, parts, starts_ref, rates_ref, end_ref, next_ref,
    state, rates, mixed, terms, sums, corr, corr_before,
    load_sem, state_send, state_recv, rate_send, rate_recv, pass_send, pass_recv,
    term_send, term_recv, sum_send, sum_recv, corr_sem, hop_sem,
):
    depth, rows, lanes = rates_ref.shape
    layers = depth * parts
    size = group_size(slabs)
    groups = slabs // size
    pair = pair_size(size, depth)
    share = depth // pair
    coarse_layers, coarse_rows = layers // 2, rows // 2
    half = coarse_layers // 2
    me, part = lax.axis_index("tm"), lax.axis_index("gz")
    group, place = me // size, lax.rem(me, size)
    wide = row_size(slabs)
    lines = slabs // wide
    line, column = me // wide, lax.rem(me, wide)
    after = lax.rem(me + 1, slabs)

    own = pl.ds(0, depth)
    rate_load = pltpu.make_async_copy(rates_ref, rates.at[own], load_sem.at[1])
    state_load = pltpu.make_async_copy(starts_ref.at[0], state.at[own], load_sem.at[0])
    rate_load.start()
    state_load.start()

    def part_at(i):
        return {"tm": me, "gz": lax.rem(part + i, parts)}

    def place_at(i):
        return {"tm": group * size + lax.rem(place + i, size), "gz": part}

    def group_at(i):
        return {"tm": lax.rem(group + i, groups) * size + place, "gz": part}

    def signal(sem, peer):
        pl.semaphore_signal(sem, inc=1, device_id=peer, device_id_type=MESH)

    def signal_beside(sem, reach):
        for d in range(1, reach + 1):
            @pl.when(line >= d)
            def _():
                signal(sem, {"tm": me - d * wide, "gz": part})

            @pl.when(line + d < lines)
            def _():
                signal(sem, {"tm": me + d * wide, "gz": part})

    def beside(reach):
        return jnp.minimum(line, reach) + jnp.minimum(lines - 1 - line, reach)

    barrier = pltpu.get_barrier_semaphore()
    near = [part_at(i) for i in range(1, parts)] + [
        {"tm": line * wide + lax.rem(column + i, wide), "gz": part} for i in range(1, wide)
    ]
    for peer in near:
        signal(barrier, peer)
    signal_beside(barrier, 1)
    pl.semaphore_wait(barrier, len(near) + beside(1))

    def remote(src, dst, send_sem, recv_sem, peer):
        return pltpu.make_async_remote_copy(
            src_ref=src, dst_ref=dst, send_sem=send_sem, recv_sem=recv_sem,
            device_id=peer, device_id_type=MESH,
        )

    def started(copy):
        copy.start()
        return copy

    mine = lax.rem(me, pair) * share
    partner = {"tm": me + 1 - 2 * lax.rem(me, pair), "gz": part}
    arrivals = [(parts - i) * depth for i in range(1, parts)]
    rate_load.wait()
    rate_copies = [
        started(remote(
            rates.at[pl.ds(mine, share)], rates.at[pl.ds(at + mine, share)],
            rate_send.at[i], rate_recv.at[i], part_at(i + 1),
        ))
        for i, at in enumerate(arrivals)
    ]
    def spread(first, last):
        for k in range(first, last):
            mixed[k] = filtered(filtered(state[k], 1, 1, fine_along_y), 1, 0, fine_along_x)

    state_load.wait()
    state_copies = [
        started(remote(
            state.at[own], state.at[pl.ds(at, depth)], state_send.at[i], state_recv.at[i], part_at(i + 1)
        ))
        for i, at in enumerate(arrivals)
    ]
    spread(0, depth)
    reaches = rounds(lines)
    for turn, reach in enumerate(reaches):
        signal_beside(hop_sem.at[turn], reach)
        if turn < len(reaches) - 1:
            pl.semaphore_wait(hop_sem.at[turn], beside(reach))

    pass_copies = []
    for i, at in enumerate(arrivals):
        rate_copies[i].wait_recv()
        if pair > 1:
            piece = rates.at[pl.ds(at + mine, share)]
            pass_copies.append(
                started(remote(piece, piece, pass_send.at[i], pass_recv.at[i], partner))
            )
    for reach in reaches[-1:]:
        pl.semaphore_wait(hop_sem.at[len(reaches) - 1], beside(reach))
    for copy in state_copies:
        copy.wait()
    spread(depth, layers)
    for copy in pass_copies:
        copy.wait()
    for copy in rate_copies:
        copy.wait_send()

    even = lax.rem(lax.broadcasted_iota(jnp.int32, (coarse_rows, lanes), 1), 2) == 0
    sides = [pl.ds(0, coarse_rows, stride=2), pl.ds(1, coarse_rows, stride=2)]

    def restricted(ref, layer):
        total = (ref[layer, sides[0], :] + ref[layer, sides[1], :]) + (
            ref[layer + 1, sides[0], :] + ref[layer + 1, sides[1], :]
        )
        pair_sum = total + jnp.where(even, turned(total, -1, 1), turned(total, 1, 1))
        return pair_sum * 0.125

    weights = [restricted(rates, 2 * k) for k in range(coarse_layers)]
    stays = [1.0 - weight for weight in weights]

    def advance(coarse):
        plane = [
            filtered(filtered(c, 2, 1, coarse_along_y), 1, 0, coarse_along_x) for c in coarse
        ]
        return [
            weights[k]
            * line_filter(
                plane[k - 1], plane[k], plane[(k + 1) % coarse_layers], coarse_along_z
            )
            + stays[k] * coarse[k]
            for k in range(coarse_layers)
        ]

    def packed_into(ref, slot, coarse):
        for k in range(half):
            ref[slot, k] = jnp.where(even, coarse[k], coarse[k + half])

    def unpacked(ref, slot):
        first, second = [], []
        for k in range(half):
            both = ref[slot, k]
            first.append(jnp.where(even, both, turned(both, 1, 1)))
            second.append(jnp.where(even, turned(both, -1, 1), both))
        return first + second

    gate = jnp.where(me > 0, 1.0, 0.0)
    guess = [gate * c for c in advance([restricted(state, 2 * k) for k in range(coarse_layers)])]

    for turn in range(FINE):
        if turn > 0:
            spread(0, layers)
        for k in range(layers):
            deep = line_filter(mixed[(k - 1) % layers], mixed[k], mixed[(k + 1) % layers], fine_along_z)
            held = state[k]
            state[k] = held + rates[k] * (deep - held)

    packed_into(terms, place, [restricted(state, 2 * k) - guess[k] for k in range(coarse_layers)])
    block = terms.at[place]
    copies = [
        started(remote(block, block, term_send.at[i - 1], term_recv.at[i - 1], place_at(i)))
        for i in range(1, size)
    ]
    for k in range(depth):
        for side in sides:
            corr[k, side, :] = state[k, side, :] - guess[k // 2]
    corr_copy = started(remote(corr, corr_before, corr_sem.at[0], corr_sem.at[1], {"tm": after, "gz": part}))

    for copy in copies:
        copy.wait()
    run = unpacked(terms, 0)
    kept = [jnp.zeros_like(c) for c in run]
    for step in range(1, size):
        kept = [jnp.where(place == step, new, old) for new, old in zip(run, kept)]
        run = [c + t for c, t in zip(advance(run), unpacked(terms, step))]
    packed_into(sums, group, run)
    block = sums.at[group]
    def sum_copy(i):
        return remote(block, block, sum_send.at[i - 1], sum_recv.at[i - 1], group_at(i))

    for i in reversed(range(1, groups)):
        @pl.when((group + i < groups) | ((group + i == groups) & (place == 0)))
        def _():
            sum_copy(i).start()

    turns = jnp.where(me == 0, groups, group)
    begun = jnp.where(turns > 0, 1.0, 0.0)

    def take(index):
        i = lax.rem(group - index + groups, groups) - 1
        held = sums.at[index]
        remote(held, held, sum_send.at[i], sum_recv.at[i], group_at(1)).wait_recv()

    def pass_group(index, coarse):
        take(index)
        coarse = list(coarse)
        for _ in range(size):
            coarse = advance(coarse)
        return tuple(c + t for c, t in zip(coarse, unpacked(sums, index)))

    @pl.when(group > 0)
    def _():
        take(0)

    coarse = tuple(begun * c for c in unpacked(sums, 0))
    coarse = lax.fori_loop(1, turns, pass_group, coarse)
    coarse = lax.fori_loop(0, place, lambda _, c: tuple(advance(list(c))), coarse)
    coarse = [c + t for c, t in zip(coarse, kept)]
    corr_copy.wait()
    before_coarse = [restricted(corr_before, 2 * k) for k in range(depth // 2)]
    finish = [gate * c for c in advance(coarse)]
    for k in range(depth):
        offset = coarse[k // 2] - before_coarse[k // 2]
        for side in sides:
            next_ref[0, k, side, :] = corr_before[k, side, :] + offset
            end_ref[0, k, side, :] = corr[k, side, :] + finish[k // 2]
    for i in range(1, groups):
        @pl.when((group + i < groups) | ((group + i == groups) & (place == 0)))
        def _():
            sum_copy(i).wait_send()


def hand_out_kernel(end_ref, next_ref, end_out, next_out, sems):
    copies = [
        pltpu.make_async_copy(end_ref, end_out, sems.at[0]),
        pltpu.make_async_copy(next_ref, next_out, sems.at[1]),
    ]
    for copy in copies:
        copy.start()
    for copy in copies:
        copy.wait()


def hand_out(end, following):
    return pl.pallas_call(
        hand_out_kernel,
        out_shape=[jax.ShapeDtypeStruct(end.shape, end.dtype)] * 2,
        in_specs=[pl.BlockSpec(memory_space=pltpu.VMEM)] * 2,
        out_specs=[pl.BlockSpec(memory_space=pl.ANY)] * 2,
        scratch_shapes=[pltpu.SemaphoreType.DMA((2,))],
    )(*(pltpu.with_memory_space_constraint(x, pltpu.VMEM) for x in (end, following)))


def solution(mesh):
    slabs, parts = mesh.shape["tm"], mesh.shape["gz"]

    def per_device(starts, cell_rates):
        depth, rows, lanes = cell_rates.shape
        layers = depth * parts
        size = group_size(slabs)
        groups = slabs // size
        whole = (layers, rows, lanes)
        packed = (layers // 4, rows // 2, lanes)
        vmem, dma = pltpu.VMEM, pltpu.SemaphoreType.DMA
        ends = pl.pallas_call(
            functools.partial(kernel, slabs, parts),
            out_shape=[pltpu.VMEM(starts.shape, jnp.float32)] * 2,
            in_specs=[pl.BlockSpec(memory_space=pl.ANY)] * 2,
            out_specs=[pl.BlockSpec(memory_space=pltpu.VMEM)] * 2,
            scratch_shapes=[
                vmem(whole, jnp.float32),
                vmem(whole, jnp.float32),
                vmem(whole, jnp.float32),
                vmem((size,) + packed, jnp.float32),
                vmem((groups,) + packed, jnp.float32),
                vmem((depth, rows, lanes), jnp.float32),
                vmem((depth, rows, lanes), jnp.float32),
                dma((2,)),
            ]
            + [dma((max(parts - 1, 1),))] * 6
            + [dma((max(size - 1, 1),))] * 2
            + [dma((max(groups - 1, 1),))] * 2
            + [dma((2,)), pltpu.SemaphoreType.REGULAR((max(len(rounds(slabs // row_size(slabs))), 1),))],
            compiler_params=pltpu.CompilerParams(collective_id=0, has_side_effects=True),
        )(starts, cell_rates)
        return hand_out(*ends)

    return jax.shard_map(
        per_device,
        mesh=mesh,
        in_specs=(P("tm", "gz", None, None), P("gz", None, None)),
        out_specs=(P("tm", "gz", None, None), P("tm", "gz", None, None)),
        check_vma=False,
    )
```

profile of v0, /device:TPU:0, one launch (start us, length us, event | category | flops | bytes accessed | tf_op | source)
XLA Modules:
  0.0 17.0 jit_solution(2210818402632210066)
XLA Ops:
  0.6 15.7 %shard_map.41 = (f32[1,4,32,128]{3,2,1,0:T(8,128)S(1)}, f32[1,4,32,128]{3,2,1,0:T(8,128)S(1)}) custom-call(f32[1,4,32,128]{3,2,1,0:T(8,128)} %starts_ref.1, f32[4,32,128]{2,1,0:T(8,128)} %rates_ref.1), custom_call_target="tpu_custom_call" | custom-call | tf_op jit(solution)/shard_map/pallas_call | solution.py:322
  16.3 0.7 %shard_map.42 = (f32[1,4,32,128]{3,2,1,0:T(8,128)}, f32[1,4,32,128]{3,2,1,0:T(8,128)}) custom-call(f32[1,4,32,128]{3,2,1,0:T(8,128)S(1)} %get-tuple-element.4.end_ref, f32[1,4,32,128]{3,2,1,0:T(8,128)S(1)} %get-tuple-element.5.next_ref), custom_call_target="tpu_custom_call" | custom-call | tf_op jit(solution)/shard_map/pallas_call | solution.py:302
where the time goes:
time: 17.1 us; the launch traced here: 17 us
  Pallas kernels  16.3 us (95%)
  between operations  0.64 us (4%)
    pallas_call x1, Pallas kernels, per_device(): pl.pallas_call(functools.partial(kernel, slabs, parts), out_shape=[pltpu....  15.7 us
    pallas_call x1, Pallas kernels, hand_out(): pl.pallas_call(hand_out_kernel, out_shape=[jax.ShapeDtypeStruct(end.shape...  0.67 us

commit v1 on v0

v1 whole, which is shorter than its diff:
```python
import functools

import jax
import jax.numpy as jnp
from jax import lax
from jax.experimental import pallas as pl
from jax.experimental.pallas import tpu as pltpu
from jax.sharding import PartitionSpec as P

MESH = pl.DeviceIdType.MESH
FINE = 4

fine_along_z = (0.1, 0.12)
fine_along_x = (0.15, 0.12)
fine_along_y = (0.2, 0.12)
coarse_along_z = (0.2, 0.25)
coarse_along_x = (0.3, 0.25)
coarse_along_y = (0.4, 0.25)


def blend(behind, middle, beyond, along):
    courant, diffuse = along
    center = 1.0 - 2.0 * diffuse
    before, after = (diffuse + 0.5 * courant) / center, (diffuse - 0.5 * courant) / center
    if middle is None:
        return before * behind if beyond is None else after * beyond
    if behind is None:
        return middle if beyond is None else middle + after * beyond
    if beyond is None:
        return middle + before * behind
    return middle + (before * behind + after * beyond)


def centers(*alongs):
    product = 1.0
    for _, diffuse in alongs:
        product *= 1.0 - 2.0 * diffuse
    return product


def turned(values, by, dim):
    return pltpu.roll(values, by % values.shape[dim], dim)


def filtered(values, by, dim, along):
    return blend(turned(values, by, dim), values, turned(values, -by, dim), along)


def kernel(
    slabs, parts, starts_ref, rates_ref, end_ref, next_ref,
    state, rates, pull, keep, mixed, field, shares, shares_in, sums, wraps, crown, crown_in,
    heads, heads_in, corr_in, parts_in,
    load_sem, ready_sem, raw_sem, rate_send, rate_recv, hand_send, hand_recv, side_send, side_recv,
    next_send, next_recv, wrap_send, wrap_recv, share_send, share_recv, sum_send, sum_recv,
    part_send, part_recv, corr_sem, head_sem, crown_send, crown_recv,
):
    depth, rows, lanes = rates_ref.shape
    layers = depth * parts
    groups = slabs // 2
    coarse_layers, coarse_rows, coarse_depth = layers // 2, rows // 2, depth // 2
    half = coarse_layers // 2
    me, part = lax.axis_index("tm"), lax.axis_index("gz")
    group, place = me // 2, lax.rem(me, 2)
    leads, helps = place == 1, place == 0
    last = group == groups - 1

    def block(r):
        return pl.ds(r % parts * depth, depth)

    own = block(0)
    rate_load = pltpu.make_async_copy(rates_ref, rates.at[own], load_sem.at[1])
    state_load = pltpu.make_async_copy(starts_ref.at[0], state.at[place, own], load_sem.at[0])
    rate_load.start()
    state_load.start()

    def leader(g, i):
        return {"tm": 2 * g + 1, "gz": lax.rem(part + i, parts)}

    def helper(g, i):
        return {"tm": 2 * g, "gz": lax.rem(part + i, parts)}

    def signal(sem, peer):
        pl.semaphore_signal(sem, inc=1, device_id=peer, device_id_type=MESH)

    def remote(src, dst, send_sem, recv_sem, peer):
        return pltpu.make_async_remote_copy(
            src_ref=src, dst_ref=dst, send_sem=send_sem, recv_sem=recv_sem,
            device_id=peer, device_id_type=MESH,
        )

    others = range(1, parts)
    barrier = pltpu.get_barrier_semaphore()
    here, far, across = ready_sem.at[0], ready_sem.at[1], ready_sem.at[2]

    @pl.when(leads)
    def _():
        for i in others:
            signal(barrier, leader(group, i))
        signal(barrier, helper(group, 0))
        for j in range(1, groups):
            @pl.when(group + j < groups)
            def _():
                signal(barrier, leader(group + j, 0))

    @pl.when(helps)
    def _():
        for i in others:
            signal(barrier, helper(group, i))

        @pl.when(group == 0)
        def _():
            for j in range(1, groups):
                for i in range(parts):
                    signal(barrier, leader(j, i))

    earlier = group + jnp.where(group > 0, parts, 0)
    pl.semaphore_wait(barrier, jnp.where(leads, parts - 1 + earlier, parts))

    def raw_copy():
        piece = state.at[0, own]
        return remote(piece, piece, raw_sem.at[0], raw_sem.at[1], leader(group, 0))

    order = sorted(range(depth), key=lambda k: min(k, depth - 1 - k))

    def rate_copy(i, k):
        return remote(
            rates.at[k], rates.at[(parts - i) * depth + k],
            rate_send.at[i - 1, k], rate_recv.at[parts - i - 1, k], leader(group, i),
        )

    def hand_copy(i):
        piece = rates.at[block(i)]
        return remote(piece, piece, hand_send.at[i - 1], hand_recv.at[i - 1], helper(group, 0))

    def side_copy(i):
        return remote(
            state.at[0, own], state.at[0, block(parts - i)],
            side_send.at[i - 1], side_recv.at[parts - i - 1], helper(group, i),
        )

    def next_copy(i):
        return remote(
            state.at[1, own], state.at[1, block(parts - i)],
            next_send.at[i], next_recv.at[(parts - i) % parts], helper(lax.rem(group + 1, groups), i),
        )

    def wrap_copy(i):
        r = (parts - i) % parts
        return remote(
            shares.at[i, 0], wraps.at[group, r], wrap_send.at[i], wrap_recv.at[group, r], helper(0, i)
        )

    def crown_copy(i):
        r = (parts - i) % parts
        return remote(crown.at[i], crown_in.at[r], crown_send.at[i], crown_recv.at[r], helper(0, i))

    def share_copy(i):
        r = parts - i - 1
        return remote(
            shares.at[i], shares_in.at[r], share_send.at[i - 1], share_recv.at[r], leader(group, i)
        )

    def sum_copy(j):
        piece = sums.at[group]
        return remote(piece, piece, sum_send.at[j - 1], sum_recv.at[group], leader(group + j, 0))

    def part_copy(i):
        r = parts - i - 1
        return remote(
            field.at[1, block(i)], parts_in.at[r], part_send.at[i - 1], part_recv.at[r], leader(group, i)
        )

    def corr_copy():
        return remote(field.at[0, own], corr_in, corr_sem.at[0], corr_sem.at[1], leader(group, 0))

    def head_copy():
        return remote(heads, heads_in, head_sem.at[0], head_sem.at[1], helper(group, 0))

    even = lax.rem(lax.broadcasted_iota(jnp.int32, (coarse_rows, lanes), 1), 2) == 0
    sides = [pl.ds(0, coarse_rows, stride=2), pl.ds(1, coarse_rows, stride=2)]
    fine_center = centers(fine_along_y, fine_along_x, fine_along_z)
    coarse_center = centers(coarse_along_y, coarse_along_x, coarse_along_z)

    def prepare(ks):
        for k in ks:
            pull[k] = rates[k] * fine_center
            keep[k] = 1.0 - rates[k]

    def restricted(ref, layer, lead=()):
        total = (ref[(*lead, layer, sides[0])] + ref[(*lead, layer, sides[1])]) + (
            ref[(*lead, layer + 1, sides[0])] + ref[(*lead, layer + 1, sides[1])]
        )
        pair_sum = total + jnp.where(even, turned(total, -1, 1), turned(total, 1, 1))
        return pair_sum * 0.125

    def coarse_rates():
        weights = [restricted(rates, 2 * k) for k in range(coarse_layers)]
        return [w * coarse_center for w in weights], [1.0 - w for w in weights]

    def plane_filtered(values, along):
        return filtered(values, 1, 0, along)

    def advance(coarse, pulls, keeps, wanted):
        plane = [
            None if c is None else plane_filtered(filtered(c, 2, 1, coarse_along_y), coarse_along_x)
            for c in coarse
        ]
        moved = [None] * coarse_layers
        for k in wanted:
            trio = plane[k - 1], plane[k], plane[(k + 1) % coarse_layers]
            if any(p is not None for p in trio):
                moved[k] = pulls[k] * across_z(trio, coarse_along_z)
                if coarse[k] is not None:
                    moved[k] = moved[k] + keeps[k] * coarse[k]
        return moved

    def across_z(trio, along):
        behind, middle, beyond = trio
        if middle is None and behind is not None and beyond is not None:
            return blend(behind, None, None, along) + blend(None, None, beyond, along)
        return blend(behind, middle, beyond, along)

    def packed(coarse, shift=0):
        def layer(k):
            return coarse[(k + shift) % coarse_layers]

        return [jnp.where(even, layer(k), layer(k + half)) for k in range(half)]

    def shifted(c):
        return {n: turned(c, n, 1) for n in (1, 2, 3, -1, -2, -3)} | {0: c}

    def mixed_lanes(t, even_by, odd_by):
        trio = [
            t[even_by + n] if even_by == odd_by else jnp.where(even, t[even_by + n], t[odd_by + n])
            for n in (2, 0, -2)
        ]
        return trio[1], plane_filtered(blend(*trio, coarse_along_y), coarse_along_x)

    def advance_packed(coarse, pulls, keeps):
        turns = [shifted(c) for c in coarse]
        plane = [mixed_lanes(t, 0, 0)[1] for t in turns]
        low, high = mixed_lanes(turns[-1], -1, 1)[1], mixed_lanes(turns[0], -1, 1)[1]
        ring = [low] + plane + [high]
        return [
            pulls[k] * blend(ring[k], ring[k + 1], ring[k + 2], coarse_along_z) + keeps[k] * coarse[k]
            for k in range(half)
        ]

    def advance_opened(coarse, pulls, keeps):
        turns = [shifted(c) for c in coarse]

        def opened(k):
            k = k % coarse_layers
            return mixed_lanes(turns[k % half], *((0, 1) if k < half else (-1, 0)))

        ring = [opened(k) for k in range(-1, coarse_depth + 1)]
        return [
            pulls[k] * blend(ring[k][1], ring[k + 1][1], ring[k + 2][1], coarse_along_z)
            + keeps[k] * ring[k + 1][0]
            for k in range(coarse_depth)
        ]

    def plus(first, second):
        return [b if a is None else a if b is None else a + b for a, b in zip(first, second)]

    def grown(ks):
        return sorted({(k + n) % layers for k in ks for n in (-1, 0, 1)})

    def spread(s, turn, ks):
        held = state if turn == 0 else field
        for k in ks:
            mixed[s, k] = plane_filtered(filtered(held[s, k], 1, 1, fine_along_y), fine_along_x)

    def settle(s, turn, live, ks):
        held = state if turn == 0 else field
        for k in ks:
            trio = [mixed[s, n % layers] if n % layers in live else None for n in (k - 1, k, k + 1)]
            value = pull[k] * across_z(trio, fine_along_z)
            field[s, k] = value + keep[k] * held[s, k] if k in live else value

    own_layers, own_coarse = list(range(depth)), list(range(coarse_depth))
    all_layers, all_coarse = list(range(layers)), list(range(coarse_layers))
    nothing = jnp.zeros((coarse_rows, lanes), jnp.float32)

    def sent_on(s, guess, ks):
        for k in ks:
            if guess[k // 2] is not None:
                for side in sides:
                    field[s, k, side, :] = field[s, k, side, :] - guess[k // 2]

    @pl.when(leads)
    def _():
        rate_load.wait()
        for k in order:
            for i in others:
                rate_copy(i, k).start()
        state_load.wait()

        @pl.when(last)
        def _():
            for i in range(parts):
                next_copy(i).start()

        prepare(own_layers)
        spread(1, 0, own_layers)
        pl.semaphore_wait(here, 1)
        for j in range(1, groups):
            @pl.when(group - j >= 0)
            def _():
                signal(far, leader(group - j, 0))

        raw_copy().wait_recv()
        spread(0, 0, own_layers)
        edges, inner = order[:2], order[2:]
        for k in edges:
            for i in others:
                rate_copy(i, k).wait_recv()
        near = [r * depth + k for r in others for k in edges]
        prepare(near)
        live, reach = own_layers, grown(own_layers)
        for s in (1, 0):
            settle(s, 0, live, reach)
        for k in inner:
            for i in others:
                rate_copy(i, k).wait_recv()
        for i in others:
            hand_copy(i).start()
        prepare([k for k in all_layers if k not in own_layers + near])
        pulls, keeps = coarse_rates()
        guesses = []
        for s, gate in ((0, jnp.where(group > 0, 1.0, 0.0)), (1, None)):
            begin = [restricted(state, 2 * k, (s,)) for k in own_coarse]
            begin = begin + [None] * (coarse_layers - coarse_depth)
            guess = advance(begin, pulls, keeps, all_coarse)
            guesses.append([g if g is None or gate is None else gate * g for g in guess])
        for turn in range(1, FINE):
            live, reach = reach, grown(reach)
            for s in (0, 1):
                spread(s, turn, live)
            for s in (0, 1):
                settle(s, turn, live, reach)
        live = reach
        for s in (0, 1):
            for k in all_layers:
                if k not in live:
                    field[s, k] = jnp.zeros((rows, lanes), jnp.float32)

        def term_of(s):
            return [
                None
                if 2 * k not in live and guesses[s][k] is None
                else restricted(field, 2 * k, (s,))
                - (nothing if guesses[s][k] is None else guesses[s][k])
                for k in all_coarse
            ]

        term, after = term_of(0), term_of(1)
        run = plus(advance(term, pulls, keeps, all_coarse), after)
        run, term = ([nothing if t is None else t for t in x] for x in (run, term))
        for i in range(parts):
            shift = i * coarse_depth
            for k, c in enumerate(packed(run, shift)):
                shares[i, 0, k] = c
            for k, c in enumerate(packed(term, shift)):
                shares[i, 1, k] = c
            for k in own_coarse:
                crown[i, k] = run[(k + shift) % coarse_layers]

        @pl.when(last)
        def _():
            for i in range(parts):
                crown_copy(i).start()

        @pl.when(~last & (group > 0))
        def _():
            for i in range(parts):
                wrap_copy(i).start()

        for i in others:
            share_copy(i).start()
        sent_on(1, guesses[1], all_layers)
        @pl.when(~last)
        def _():
            pl.semaphore_wait(far, groups - 1 - group)

        for i in others:
            signal(across, leader(group, i))
        total, middle = packed(run), packed(term)
        for r in others:
            share_copy(parts - r).wait_recv()
            total = plus(total, [shares_in[r - 1, 0, k] for k in range(half)])
            middle = plus(middle, [shares_in[r - 1, 1, k] for k in range(half)])
        for k in range(half):
            sums[group, k] = total[k]
        for j in reversed(range(1, groups)):
            @pl.when(group + j < groups)
            def _():
                sum_copy(j).start()

        if parts > 1:
            pl.semaphore_wait(across, parts - 1)

        @pl.when(group == 0)
        def _():
            for i in range(parts):
                wrap_copy(i).start()

        @pl.when(~last)
        def _():
            for i in range(parts):
                next_copy(i).start()

        for i in others:
            part_copy(i).start()

        packed_pulls, packed_keeps = packed(pulls), packed(keeps)

        def take(index):
            piece = sums.at[index]
            remote(piece, piece, sum_send.at[0], sum_recv.at[index], leader(group, 1)).wait_recv()

        @pl.when(group > 0)
        def _():
            take(0)

        begun = jnp.where(group > 0, 1.0, 0.0)
        coarse = tuple(begun * sums[0, k] for k in range(half))

        def pass_group(index, coarse):
            for _ in range(2):
                coarse = advance_packed(coarse, packed_pulls, packed_keeps)
            take(index)
            return tuple(plus(coarse, [sums[index, k] for k in range(half)]))

        coarse = list(lax.fori_loop(1, jnp.maximum(group, 1), pass_group, coarse))
        ahead = advance_opened(coarse, pulls, keeps)
        opened = []
        for k in own_coarse:
            both = coarse[k % half]
            opened.append(
                jnp.where(even, both, turned(both, 1, 1))
                if k < half
                else jnp.where(even, turned(both, -1, 1), both)
            )
        for k in own_coarse:
            heads[0, k] = opened[k]
            heads[1, k] = ahead[k]

        @pl.when(group > 0)
        def _():
            head_copy().start()

        finish = advance_opened(
            plus(advance_packed(coarse, packed_pulls, packed_keeps), middle), pulls, keeps
        )
        corr_copy().wait_recv()
        for r in others:
            part_copy(parts - r).wait_recv()
        for k in own_layers:
            for side in sides:
                next_ref[0, k, side, :] = corr_in[k, side, :] + ahead[k // 2]
                held = field[1, k, side, :]
                for r in others:
                    held = held + parts_in[r - 1, k, side, :]
                end_ref[0, k, side, :] = held + finish[k // 2]
        for i in others:
            for k in order:
                rate_copy(i, k).wait_send()
            hand_copy(i).wait_send()
            share_copy(i).wait_send()
            part_copy(i).wait_send()
        for i in range(parts):
            next_copy(i).wait_send()
        for j in range(1, groups):
            @pl.when(group + j < groups)
            def _():
                sum_copy(j).wait_send()

        @pl.when(last)
        def _():
            for i in range(parts):
                crown_copy(i).wait_send()

        @pl.when(~last)
        def _():
            for i in range(parts):
                wrap_copy(i).wait_send()

        @pl.when(group > 0)
        def _():
            head_copy().wait_send()

    @pl.when(helps)
    def _():
        signal(here, leader(group, 0))
        state_load.wait()
        raw_copy().start()
        rate_load.wait()
        prepare(own_layers)
        raw_copy().wait_send()
        for i in others:
            side_copy(i).start()
        for i in others:
            side_copy(i).wait_recv()
            hand_copy(i).wait_recv()
        prepare([k for k in all_layers if k not in own_layers])
        pulls, keeps = coarse_rates()

        def solve(s, gate):
            begin = [restricted(state, 2 * k, (s,)) for k in all_coarse]
            guess = advance(begin, pulls, keeps, own_coarse)
            if gate is not None:
                guess = [g if g is None else gate * g for g in guess]
            wanted = [own_layers]
            for _ in range(1, FINE):
                wanted.append(grown(wanted[-1]))
            for turn in range(FINE):
                reach = wanted[FINE - 1 - turn]
                spread(s, turn, grown(reach))
                settle(s, turn, all_layers, reach)
            sent_on(s, guess, own_layers)

        solve(0, jnp.where(group > 0, 1.0, 0.0))
        corr_copy().start()
        for r in range(parts):
            next_copy(r).wait_recv()
        solve(1, None)
        before = [restricted(field, 2 * k, (1,)) for k in own_coarse]
        for k in own_layers:
            for side in sides:
                next_ref[0, k, side, :] = field[1, k, side, :] - before[k // 2]
                end_ref[0, k, side, :] = field[0, k, side, :]

        @pl.when(group == 0)
        def _():
            packed_pulls, packed_keeps = packed(pulls), packed(keeps)

            def pass_group(index, coarse):
                for _ in range(2):
                    coarse = advance_packed(coarse, packed_pulls, packed_keeps)
                for r in range(parts):
                    piece = wraps.at[index, r]
                    remote(
                        piece, piece, wrap_send.at[0], wrap_recv.at[index, r], leader(0, 0)
                    ).wait_recv()
                    coarse = plus(coarse, [wraps[index, r, k] for k in range(half)])
                return tuple(coarse)

            coarse = list(lax.fori_loop(0, groups - 1, pass_group, (nothing,) * half))
            coarse = advance_packed(coarse, packed_pulls, packed_keeps)
            coarse = advance_opened(coarse, pulls, keeps)
            for k in own_layers:
                for side in sides:
                    next_ref[0, k, side, :] = next_ref[0, k, side, :] + coarse[k // 2]
            for r in range(parts):
                crown_copy((parts - r) % parts).wait_recv()
            for k in own_layers:
                offset = crown_in[0, k // 2]
                for r in others:
                    offset = offset + crown_in[r, k // 2]
                for side in sides:
                    next_ref[0, k, side, :] = next_ref[0, k, side, :] + offset

        @pl.when(group > 0)
        def _():
            head_copy().wait_recv()
            for k in own_layers:
                for side in sides:
                    next_ref[0, k, side, :] = next_ref[0, k, side, :] + heads_in[0, k // 2]
                    end_ref[0, k, side, :] = end_ref[0, k, side, :] + heads_in[1, k // 2]

        corr_copy().wait_send()
        for i in others:
            side_copy(i).wait_send()


def hand_out_kernel(end_ref, next_ref, end_out, next_out, sems):
    copies = [
        pltpu.make_async_copy(end_ref, end_out, sems.at[0]),
        pltpu.make_async_copy(next_ref, next_out, sems.at[1]),
    ]
    for copy in copies:
        copy.start()
    for copy in copies:
        copy.wait()


def hand_out(end, following):
    return pl.pallas_call(
        hand_out_kernel,
        out_shape=[jax.ShapeDtypeStruct(end.shape, end.dtype)] * 2,
        in_specs=[pl.BlockSpec(memory_space=pltpu.VMEM)] * 2,
        out_specs=[pl.BlockSpec(memory_space=pl.ANY)] * 2,
        scratch_shapes=[pltpu.SemaphoreType.DMA((2,))],
    )(*(pltpu.with_memory_space_constraint(x, pltpu.VMEM) for x in (end, following)))


def solution(mesh):
    slabs, parts = mesh.shape["tm"], mesh.shape["gz"]

    def per_device(starts, cell_rates):
        depth, rows, lanes = cell_rates.shape
        layers = depth * parts
        groups = slabs // 2
        packed = (layers // 4, rows // 2, lanes)
        lead = (depth // 2, rows // 2, lanes)
        aside = max(parts - 1, 1)
        dma = pltpu.SemaphoreType.DMA

        def vmem(*shape):
            return pltpu.VMEM(shape, jnp.float32)

        ends = pl.pallas_call(
            functools.partial(kernel, slabs, parts),
            out_shape=[pltpu.VMEM(starts.shape, jnp.float32)] * 2,
            in_specs=[pl.BlockSpec(memory_space=pl.ANY)] * 2,
            out_specs=[pl.BlockSpec(memory_space=pltpu.VMEM)] * 2,
            scratch_shapes=[
                vmem(2, layers, rows, lanes),
                vmem(layers, rows, lanes),
                vmem(layers, rows, lanes),
                vmem(layers, rows, lanes),
                vmem(2, layers, rows, lanes),
                vmem(2, layers, rows, lanes),
                vmem(parts, 2, *packed),
                vmem(aside, 2, *packed),
                vmem(groups, *packed),
                vmem(groups, parts, *packed),
                vmem(parts, *lead),
                vmem(parts, *lead),
                vmem(2, *lead),
                vmem(2, *lead),
                vmem(depth, rows, lanes),
                vmem(aside, depth, rows, lanes),
                dma((2,)),
                pltpu.SemaphoreType.REGULAR((3,)),
                dma((2,)),
            ]
            + [dma((aside, depth))] * 2
            + [dma((aside,))] * 4
            + [dma((parts,))] * 2
            + [dma((parts,)), dma((groups, parts))]
            + [dma((aside,))] * 2
            + [dma((max(groups - 1, 1),)), dma((groups,))]
            + [dma((aside,))] * 2
            + [dma((2,))] * 2
            + [dma((parts,))] * 2,
            compiler_params=pltpu.CompilerParams(collective_id=0, has_side_effects=True),
        )(starts, cell_rates)
        return hand_out(*ends)

    return jax.shard_map(
        per_device,
        mesh=mesh,
        in_specs=(P("tm", "gz", None, None), P("gz", None, None)),
        out_specs=(P("tm", "gz", None, None), P("tm", "gz", None, None)),
        check_vma=False,
    )
```

time: 17.1 us -> 14.7 us (0.86)
  Pallas kernels: 16.3 us -> 13.9 us
    pallas_call x1, Pallas kernels: 15.7 us -> 13.2 us  [per_device(): pl.pallas_call(functools.partial(kernel, slabs, parts), out_shape=[pltpu....]
where the time goes in v1:
time: 14.7 us; the launch traced here: 14.5 us
  Pallas kernels  13.9 us (95%)
  between operations  0.64 us (4%)
    pallas_call x1, Pallas kernels, per_device(): pl.pallas_call(functools.partial(kernel, slabs, parts), out_shape=[pltpu....  13.2 us
    pallas_call x1, Pallas kernels, hand_out(): pl.pallas_call(hand_out_kernel, out_shape=[jax.ShapeDtypeStruct(end.shape...  0.67 us

profile of v1, /device:TPU:0, one launch (start us, length us, event | category | flops | bytes accessed | tf_op | source)
XLA Modules:
  0.0 14.5 jit_solution(304569547046762376)
XLA Ops:
  0.6 13.2 %shard_map.41 = (f32[1,4,32,128]{3,2,1,0:T(8,128)S(1)}, f32[1,4,32,128]{3,2,1,0:T(8,128)S(1)}) custom-call(f32[1,4,32,128]{3,2,1,0:T(8,128)} %starts_ref.1, f32[4,32,128]{2,1,0:T(8,128)} %rates_ref.1), custom_call_target="tpu_custom_call" | custom-call | tf_op jit(solution)/shard_map/pallas_call | solution.py:613
  13.8 0.7 %shard_map.42 = (f32[1,4,32,128]{3,2,1,0:T(8,128)}, f32[1,4,32,128]{3,2,1,0:T(8,128)}) custom-call(f32[1,4,32,128]{3,2,1,0:T(8,128)S(1)} %get-tuple-element.4.end_ref, f32[1,4,32,128]{3,2,1,0:T(8,128)S(1)} %get-tuple-element.5.next_ref), custom_call_target="tpu_custom_call" | custom-call | tf_op jit(solution)/shard_map/pallas_call | solution.py:589

commit v2 on v1

--- a/solution.py
+++ b/solution.py
@@ -50,9 +50,7 @@
     slabs, parts, starts_ref, rates_ref, end_ref, next_ref,
     state, rates, pull, keep, mixed, field, shares, shares_in, sums, wraps, crown, crown_in,
     heads, heads_in, corr_in, parts_in,
-    load_sem, ready_sem, raw_sem, rate_send, rate_recv, hand_send, hand_recv, side_send, side_recv,
-    next_send, next_recv, wrap_send, wrap_recv, share_send, share_recv, sum_send, sum_recv,
-    part_send, part_recv, corr_sem, head_sem, crown_send, crown_recv,
+    ready, leave, arrive,
 ):
     depth, rows, lanes = rates_ref.shape
     layers = depth * parts
@@ -68,8 +66,8 @@
         return pl.ds(r % parts * depth, depth)
 
     own = block(0)
-    rate_load = pltpu.make_async_copy(rates_ref, rates.at[own], load_sem.at[1])
-    state_load = pltpu.make_async_copy(starts_ref.at[0], state.at[place, own], load_sem.at[0])
+    rate_load = pltpu.make_async_copy(rates_ref, rates.at[own], leave.at[5])
+    state_load = pltpu.make_async_copy(starts_ref.at[0], state.at[place, own], leave.at[6])
     rate_load.start()
     state_load.start()
 
@@ -90,7 +88,8 @@
 
     others = range(1, parts)
     barrier = pltpu.get_barrier_semaphore()
-    here, far, across = ready_sem.at[0], ready_sem.at[1], ready_sem.at[2]
+    here, near_open, far_open, across = (ready.at[n] for n in range(4))
+    line = 6
 
     @pl.when(leads)
     def _():
@@ -116,65 +115,66 @@
     earlier = group + jnp.where(group > 0, parts, 0)
     pl.semaphore_wait(barrier, jnp.where(leads, parts - 1 + earlier, parts))
 
+    def drain(sem, ref):
+        pltpu.make_async_copy(ref, ref, sem).wait()
+
     def raw_copy():
         piece = state.at[0, own]
-        return remote(piece, piece, raw_sem.at[0], raw_sem.at[1], leader(group, 0))
+        return remote(piece, piece, leave.at[0], arrive.at[0], leader(group, 0))
 
     order = sorted(range(depth), key=lambda k: min(k, depth - 1 - k))
+    edges, inner = order[:2], order[2:]
 
     def rate_copy(i, k):
         return remote(
             rates.at[k], rates.at[(parts - i) * depth + k],
-            rate_send.at[i - 1, k], rate_recv.at[parts - i - 1, k], leader(group, i),
+            leave.at[0], arrive.at[1 if k in edges else 2], leader(group, i),
         )
 
     def hand_copy(i):
         piece = rates.at[block(i)]
-        return remote(piece, piece, hand_send.at[i - 1], hand_recv.at[i - 1], helper(group, 0))
+        return remote(piece, piece, leave.at[1], arrive.at[1], helper(group, 0))
 
     def side_copy(i):
         return remote(
-            state.at[0, own], state.at[0, block(parts - i)],
-            side_send.at[i - 1], side_recv.at[parts - i - 1], helper(group, i),
+            state.at[0, own], state.at[0, block(parts - i)], leave.at[1], arrive.at[2], helper(group, i)
         )
 
     def next_copy(i):
         return remote(
-            state.at[1, own], state.at[1, block(parts - i)],
-            next_send.at[i], next_recv.at[(parts - i) % parts], helper(lax.rem(group + 1, groups), i),
+            state.at[1, own], state.at[1, block(parts - i)], leave.at[2], arrive.at[0],
+            helper(lax.rem(group + 1, groups), i),
         )
 
     def wrap_copy(i):
-        r = (parts - i) % parts
         return remote(
-            shares.at[i, 0], wraps.at[group, r], wrap_send.at[i], wrap_recv.at[group, r], helper(0, i)
+            shares.at[i, 0], wraps.at[group, (parts - i) % parts], leave.at[3], arrive.at[line + group],
+            helper(0, i),
         )
 
     def crown_copy(i):
-        r = (parts - i) % parts
-        return remote(crown.at[i], crown_in.at[r], crown_send.at[i], crown_recv.at[r], helper(0, i))
+        return remote(
+            crown.at[i], crown_in.at[(parts - i) % parts], leave.at[3], arrive.at[line + group],
+            helper(0, i),
+        )
 
     def share_copy(i):
-        r = parts - i - 1
-        return remote(
-            shares.at[i], shares_in.at[r], share_send.at[i - 1], share_recv.at[r], leader(group, i)
-        )
+        return remote(shares.at[i], shares_in.at[parts - i - 1], leave.at[4], arrive.at[3], leader(group, i))
 
     def sum_copy(j):
         piece = sums.at[group]
-        return remote(piece, piece, sum_send.at[j - 1], sum_recv.at[group], leader(group + j, 0))
+        return remote(piece, piece, leave.at[7], arrive.at[line + group], leader(group + j, 0))
 
     def part_copy(i):
-        r = parts - i - 1
         return remote(
-            field.at[1, block(i)], parts_in.at[r], part_send.at[i - 1], part_recv.at[r], leader(group, i)
+            field.at[1, block(i)], parts_in.at[parts - i - 1], leave.at[5], arrive.at[4], leader(group, i)
         )
 
     def corr_copy():
-        return remote(field.at[0, own], corr_in, corr_sem.at[0], corr_sem.at[1], leader(group, 0))
+        return remote(field.at[0, own], corr_in, leave.at[2], arrive.at[5], leader(group, 0))
 
     def head_copy():
-        return remote(heads, heads_in, head_sem.at[0], head_sem.at[1], helper(group, 0))
+        return remote(heads, heads_in, leave.at[6], arrive.at[3], helper(group, 0))
 
     even = lax.rem(lax.broadcasted_iota(jnp.int32, (coarse_rows, lanes), 1), 2) == 0
     sides = [pl.ds(0, coarse_rows, stride=2), pl.ds(1, coarse_rows, stride=2)]
@@ -291,7 +291,7 @@
     @pl.when(leads)
     def _():
         rate_load.wait()
-        for k in order:
+        for k in edges:
             for i in others:
                 rate_copy(i, k).start()
         state_load.wait()
@@ -302,29 +302,36 @@
                 next_copy(i).start()
 
         prepare(own_layers)
+        for k in inner:
+            for i in others:
+                rate_copy(i, k).start()
         spread(1, 0, own_layers)
         pl.semaphore_wait(here, 1)
         for j in range(1, groups):
             @pl.when(group - j >= 0)
             def _():
-                signal(far, leader(group - j, 0))
+                signal(near_open if j == 1 else far_open, leader(group - j, 0))
 
         raw_copy().wait_recv()
         spread(0, 0, own_layers)
-        edges, inner = order[:2], order[2:]
-        for k in edges:
-            for i in others:
-                rate_copy(i, k).wait_recv()
+        drain(arrive.at[1], rates.at[pl.ds(0, len(edges) * (parts - 1))])
         near = [r * depth + k for r in others for k in edges]
         prepare(near)
         live, reach = own_layers, grown(own_layers)
         for s in (1, 0):
             settle(s, 0, live, reach)
-        for k in inner:
-            for i in others:
-                rate_copy(i, k).wait_recv()
+        if inner:
+            drain(arrive.at[2], rates.at[pl.ds(0, len(inner) * (parts - 1))])
         for i in others:
             hand_copy(i).start()
+
+        @pl.when(~last)
+        def _():
+            pl.semaphore_wait(near_open, 1)
+            for i in others:
+                signal(across, leader(group, i))
+            next_copy(0).start()
+
         prepare([k for k in all_layers if k not in own_layers + near])
         pulls, keeps = coarse_rates()
         guesses = []
@@ -368,26 +375,38 @@
 
         @pl.when(last)
         def _():
-            for i in range(parts):
+            for i in reversed(range(parts)):
                 crown_copy(i).start()
 
         @pl.when(~last & (group > 0))
+        def _():
+            for i in reversed(range(parts)):
+                wrap_copy(i).start()
+
+        for i in others:
+            share_copy(i).start()
+
+        @pl.when(~last)
+        def _():
+            if parts > 1:
+                pl.semaphore_wait(across, parts - 1)
+            for i in others:
+                next_copy(i).start()
+
+        @pl.when(group == 0)
         def _():
             for i in range(parts):
                 wrap_copy(i).start()
 
-        for i in others:
-            share_copy(i).start()
         sent_on(1, guesses[1], all_layers)
-        @pl.when(~last)
-        def _():
-            pl.semaphore_wait(far, groups - 1 - group)
-
-        for i in others:
-            signal(across, leader(group, i))
+
+        @pl.when(group + 2 < groups)
+        def _():
+            pl.semaphore_wait(far_open, groups - 2 - group)
+
         total, middle = packed(run), packed(term)
+        drain(arrive.at[3], shares_in)
         for r in others:
-            share_copy(parts - r).wait_recv()
             total = plus(total, [shares_in[r - 1, 0, k] for k in range(half)])
             middle = plus(middle, [shares_in[r - 1, 1, k] for k in range(half)])
         for k in range(half):
@@ -397,27 +416,13 @@
             def _():
                 sum_copy(j).start()
 
-        if parts > 1:
-            pl.semaphore_wait(across, parts - 1)
-
-        @pl.when(group == 0)
-        def _():
-            for i in range(parts):
-                wrap_copy(i).start()
-
-        @pl.when(~last)
-        def _():
-            for i in range(parts):
-                next_copy(i).start()
-
         for i in others:
             part_copy(i).start()
 
         packed_pulls, packed_keeps = packed(pulls), packed(keeps)
 
         def take(index):
-            piece = sums.at[index]
-            remote(piece, piece, sum_send.at[0], sum_recv.at[index], leader(group, 1)).wait_recv()
+            drain(arrive.at[line + index], sums.at[index])
 
         @pl.when(group > 0)
         def _():
@@ -454,8 +459,7 @@
             plus(advance_packed(coarse, packed_pulls, packed_keeps), middle), pulls, keeps
         )
         corr_copy().wait_recv()
-        for r in others:
-            part_copy(parts - r).wait_recv()
+        drain(arrive.at[4], parts_in)
         for k in own_layers:
             for side in sides:
                 next_ref[0, k, side, :] = corr_in[k, side, :] + ahead[k // 2]
@@ -463,32 +467,28 @@
                 for r in others:
                     held = held + parts_in[r - 1, k, side, :]
                 end_ref[0, k, side, :] = held + finish[k // 2]
-        for i in others:
-            for k in order:
-                rate_copy(i, k).wait_send()
-            hand_copy(i).wait_send()
-            share_copy(i).wait_send()
-            part_copy(i).wait_send()
-        for i in range(parts):
-            next_copy(i).wait_send()
+        away = pl.ds(0, depth * (parts - 1))
+        drain(leave.at[0], rates.at[away])
+        drain(leave.at[1], rates.at[away])
+        drain(leave.at[2], state.at[1])
+        drain(leave.at[4], shares_in)
+        drain(leave.at[5], parts_in)
         for j in range(1, groups):
-            @pl.when(group + j < groups)
+            @pl.when(groups - 1 - group == j)
             def _():
-                sum_copy(j).wait_send()
+                drain(leave.at[7], sums.at[pl.ds(0, j)])
 
         @pl.when(last)
         def _():
-            for i in range(parts):
-                crown_copy(i).wait_send()
+            drain(leave.at[3], crown_in)
 
         @pl.when(~last)
         def _():
-            for i in range(parts):
-                wrap_copy(i).wait_send()
+            drain(leave.at[3], wraps.at[0])
 
         @pl.when(group > 0)
         def _():
-            head_copy().wait_send()
+            drain(leave.at[6], heads)
 
     @pl.when(helps)
     def _():
@@ -500,9 +500,9 @@
         raw_copy().wait_send()
         for i in others:
             side_copy(i).start()
-        for i in others:
-            side_copy(i).wait_recv()
-            hand_copy(i).wait_recv()
+        away = pl.ds(0, depth * (parts - 1))
+        drain(arrive.at[2], rates.at[away])
+        drain(arrive.at[1], rates.at[away])
         prepare([k for k in all_layers if k not in own_layers])
         pulls, keeps = coarse_rates()
 
@@ -522,8 +522,25 @@
 
         solve(0, jnp.where(group > 0, 1.0, 0.0))
         corr_copy().start()
-        for r in range(parts):
-            next_copy(r).wait_recv()
+
+        def pass_group(index, coarse):
+            for _ in range(2):
+                coarse = advance_packed(coarse, packed_pulls, packed_keeps)
+            drain(arrive.at[line + index], wraps.at[index])
+            for r in range(parts):
+                coarse = plus(coarse, [wraps[index, r, k] for k in range(half)])
+            return tuple(coarse)
+
+        packed_pulls, packed_keeps = packed(pulls), packed(keeps)
+        midway = groups // 2
+
+        @pl.when(group == 0)
+        def _():
+            coarse = lax.fori_loop(0, midway, pass_group, (nothing,) * half)
+            for k in range(half):
+                sums[0, k] = coarse[k]
+
+        drain(arrive.at[0], state.at[1])
         solve(1, None)
         before = [restricted(field, 2 * k, (1,)) for k in own_coarse]
         for k in own_layers:
@@ -533,27 +550,14 @@
 
         @pl.when(group == 0)
         def _():
-            packed_pulls, packed_keeps = packed(pulls), packed(keeps)
-
-            def pass_group(index, coarse):
-                for _ in range(2):
-                    coarse = advance_packed(coarse, packed_pulls, packed_keeps)
-                for r in range(parts):
-                    piece = wraps.at[index, r]
-                    remote(
-                        piece, piece, wrap_send.at[0], wrap_recv.at[index, r], leader(0, 0)
-                    ).wait_recv()
-                    coarse = plus(coarse, [wraps[index, r, k] for k in range(half)])
-                return tuple(coarse)
-
-            coarse = list(lax.fori_loop(0, groups - 1, pass_group, (nothing,) * half))
+            coarse = tuple(sums[0, k] for k in range(half))
+            coarse = lax.fori_loop(midway, groups - 1, pass_group, coarse)
             coarse = advance_packed(coarse, packed_pulls, packed_keeps)
             coarse = advance_opened(coarse, pulls, keeps)
             for k in own_layers:
                 for side in sides:
                     next_ref[0, k, side, :] = next_ref[0, k, side, :] + coarse[k // 2]
-            for r in range(parts):
-                crown_copy((parts - r) % parts).wait_recv()
+            drain(arrive.at[line + groups - 1], crown_in)
             for k in own_layers:
                 offset = crown_in[0, k // 2]
                 for r in others:
@@ -569,9 +573,8 @@
                     next_ref[0, k, side, :] = next_ref[0, k, side, :] + heads_in[0, k // 2]
                     end_ref[0, k, side, :] = end_ref[0, k, side, :] + heads_in[1, k // 2]
 
-        corr_copy().wait_send()
-        for i in others:
-            side_copy(i).wait_send()
+        drain(leave.at[2], corr_in)
+        drain(leave.at[1], rates.at[away])
 
 
 def hand_out_kernel(end_ref, next_ref, end_out, next_out, sems):
@@ -632,19 +635,10 @@
                 vmem(2, *lead),
                 vmem(depth, rows, lanes),
                 vmem(aside, depth, rows, lanes),
-                dma((2,)),
-                pltpu.SemaphoreType.REGULAR((3,)),
-                dma((2,)),
-            ]
-            + [dma((aside, depth))] * 2
-            + [dma((aside,))] * 4
-            + [dma((parts,))] * 2
-            + [dma((parts,)), dma((groups, parts))]
-            + [dma((aside,))] * 2
-            + [dma((max(groups - 1, 1),)), dma((groups,))]
-            + [dma((aside,))] * 2
-            + [dma((2,))] * 2
-            + [dma((parts,))] * 2,
+                pltpu.SemaphoreType.REGULAR((4,)),
+                dma((8,)),
+                dma((6 + groups,)),
+            ],
             compiler_params=pltpu.CompilerParams(collective_id=0, has_side_effects=True),
         )(starts, cell_rates)
         return hand_out(*ends)

time: 14.7 us -> 14.4 us (0.980)
  Pallas kernels: 13.9 us -> 13.6 us
    pallas_call x1, Pallas kernels: 13.2 us -> 12.9 us  [per_device(): pl.pallas_call(functools.partial(kernel, slabs, parts), out_shape=[pltpu....]
where the time goes in v2:
time: 14.4 us; the launch traced here: 14.2 us
  Pallas kernels  13.6 us (94%)
  between operations  0.64 us (4%)
    pallas_call x1, Pallas kernels, per_device(): pl.pallas_call(functools.partial(kernel, slabs, parts), out_shape=[pltpu....  12.9 us
    pallas_call x1, Pallas kernels, hand_out(): pl.pallas_call(hand_out_kernel, out_shape=[jax.ShapeDtypeStruct(end.shape...  0.67 us

profile of v2, /device:TPU:0, one launch (start us, length us, event | category | flops | bytes accessed | tf_op | source)
XLA Modules:
  0.0 14.2 jit_solution(16304399692339600569)
XLA Ops:
  0.6 12.9 %shard_map.41 = (f32[1,4,32,128]{3,2,1,0:T(8,128)S(1)}, f32[1,4,32,128]{3,2,1,0:T(8,128)S(1)}) custom-call(f32[1,4,32,128]{3,2,1,0:T(8,128)} %starts_ref.1, f32[4,32,128]{2,1,0:T(8,128)} %rates_ref.1), custom_call_target="tpu_custom_call" | custom-call | tf_op jit(solution)/shard_map/pallas_call | solution.py:616
  13.6 0.7 %shard_map.42 = (f32[1,4,32,128]{3,2,1,0:T(8,128)}, f32[1,4,32,128]{3,2,1,0:T(8,128)}) custom-call(f32[1,4,32,128]{3,2,1,0:T(8,128)S(1)} %get-tuple-element.4.end_ref, f32[1,4,32,128]{3,2,1,0:T(8,128)S(1)} %get-tuple-element.5.next_ref), custom_call_target="tpu_custom_call" | custom-call | tf_op jit(solution)/shard_map/pallas_call | solution.py:592

commit v3 on v2

v3 whole, which is shorter than its diff:
```python
import functools

import jax
import jax.numpy as jnp
from jax import lax
from jax.experimental import pallas as pl
from jax.experimental.pallas import tpu as pltpu
from jax.sharding import PartitionSpec as P

MESH = pl.DeviceIdType.MESH
FINE = 4
SUBLANES = 8

fine_along_z = (0.1, 0.12)
fine_along_x = (0.15, 0.12)
fine_along_y = (0.2, 0.12)
coarse_along_z = (0.2, 0.25)
coarse_along_x = (0.3, 0.25)
coarse_along_y = (0.4, 0.25)


def blend(behind, middle, beyond, along):
    courant, diffuse = along
    center = 1.0 - 2.0 * diffuse
    before, after = (diffuse + 0.5 * courant) / center, (diffuse - 0.5 * courant) / center
    if middle is None:
        return before * behind if beyond is None else after * beyond
    if behind is None:
        return middle if beyond is None else middle + after * beyond
    if beyond is None:
        return middle + before * behind
    return middle + (before * behind + after * beyond)


def centers(*alongs):
    product = 1.0
    for _, diffuse in alongs:
        product *= 1.0 - 2.0 * diffuse
    return product


def turned(values, by, dim):
    return pltpu.roll(values, by % values.shape[dim], dim)


def lane_filtered(values, by, along):
    return blend(turned(values, by, 1), values, turned(values, -by, 1), along)


def row_filtered(plane, along):
    ring = (turned(plane[-1], 1, 0), *plane, turned(plane[0], -1, 0))
    return tuple(blend(*ring[j : j + 3], along) for j in range(len(plane)))


def each(f, *planes):
    return tuple(f(*vectors) for vectors in zip(*planes))


def kernel(
    slabs, parts, starts_ref, rates_ref, end_ref, next_ref,
    state, rates, pull, keep, mixed, field, shares, shares_in, sums, wraps, crown, crown_in,
    heads, heads_in, corr_in, parts_in, base,
    ready, leave, arrive,
):
    depth, rows, lanes = rates_ref.shape
    layers = depth * parts
    groups = slabs // 2
    coarse_layers, coarse_rows, coarse_depth = layers // 2, rows // 2, depth // 2
    half = coarse_layers // 2
    vectors = rows // SUBLANES
    coarse_vectors = vectors // 2
    me, part = lax.axis_index("tm"), lax.axis_index("gz")
    group, place = me // 2, lax.rem(me, 2)
    leads, helps = place == 1, place == 0
    last = group == groups - 1

    def block(r):
        return pl.ds(r % parts * depth, depth)

    own = block(0)
    rate_load = pltpu.make_async_copy(rates_ref, rates.at[own], leave.at[5])
    state_load = pltpu.make_async_copy(starts_ref.at[0], state.at[place, own], leave.at[6])
    rate_load.start()
    state_load.start()

    def leader(g, i):
        return {"tm": 2 * g + 1, "gz": lax.rem(part + i, parts)}

    def helper(g, i):
        return {"tm": 2 * g, "gz": lax.rem(part + i, parts)}

    def signal(sem, peer):
        pl.semaphore_signal(sem, inc=1, device_id=peer, device_id_type=MESH)

    def remote(src, dst, send_sem, recv_sem, peer):
        return pltpu.make_async_remote_copy(
            src_ref=src, dst_ref=dst, send_sem=send_sem, recv_sem=recv_sem,
            device_id=peer, device_id_type=MESH,
        )

    others = range(1, parts)
    barrier = pltpu.get_barrier_semaphore()
    here, near_open, far_open, across = (ready.at[n] for n in range(4))
    line = 7

    @pl.when(leads)
    def _():
        for i in others:
            signal(barrier, leader(group, i))
        signal(barrier, helper(group, 0))
        for j in range(1, groups):
            @pl.when(group + j < groups)
            def _():
                signal(barrier, leader(group + j, 0))

    @pl.when(helps)
    def _():
        for i in others:
            signal(barrier, helper(group, i))

        @pl.when(group == 0)
        def _():
            for j in range(1, groups):
                for i in range(parts):
                    signal(barrier, leader(j, i))

    earlier = group + jnp.where(group > 0, parts, 0)
    pl.semaphore_wait(barrier, jnp.where(leads, parts - 1 + earlier, parts))

    def drain(sem, ref):
        pltpu.make_async_copy(ref, ref, sem).wait()

    def raw_copy():
        piece = state.at[0, own]
        return remote(piece, piece, leave.at[0], arrive.at[0], leader(group, 0))

    def rate_copy(i):
        return remote(
            rates.at[own], rates.at[block(parts - i)],
            leave.at[0], arrive.at[1], leader(group, i),
        )

    def hand_copy(i):
        piece = rates.at[block(i)]
        return remote(piece, piece, leave.at[1], arrive.at[1], helper(group, 0))

    def side_copy(i):
        return remote(
            state.at[0, own], state.at[0, block(parts - i)], leave.at[1], arrive.at[2], helper(group, i)
        )

    def next_copy(i):
        return remote(
            state.at[1, own], state.at[1, block(parts - i)], leave.at[2], arrive.at[0],
            helper(lax.rem(group + 1, groups), i),
        )

    def wrap_copy(i):
        return remote(
            shares.at[i, 0], wraps.at[group, (parts - i) % parts], leave.at[3], arrive.at[line + group],
            helper(0, i),
        )

    def first_copy():
        return remote(sums.at[0], wraps.at[0, 0], leave.at[3], arrive.at[line], helper(0, 0))

    def crown_copy(i):
        return remote(
            crown.at[i], crown_in.at[(parts - i) % parts], leave.at[3], arrive.at[line + group],
            helper(0, i),
        )

    def share_copy(i, n):
        return remote(
            shares.at[i, n], shares_in.at[n, parts - i - 1], leave.at[4 if n == 0 else 8],
            arrive.at[3 if n == 0 else 6], leader(group, i),
        )

    def sum_copy(j):
        piece = sums.at[group]
        return remote(piece, piece, leave.at[7], arrive.at[line + group], leader(group + j, 0))

    def part_copy(i):
        return remote(
            field.at[1, block(i)], parts_in.at[parts - i - 1], leave.at[5], arrive.at[4], leader(group, i)
        )

    def corr_copy():
        return remote(field.at[0, own], corr_in, leave.at[2], arrive.at[5], leader(group, 0))

    def head_copy():
        return remote(heads, heads_in, leave.at[6], arrive.at[3], helper(group, 0))

    even = lax.rem(lax.broadcasted_iota(jnp.int32, (SUBLANES, lanes), 1), 2) == 0
    fine_center = centers(fine_along_y, fine_along_x, fine_along_z)
    coarse_center = centers(coarse_along_y, coarse_along_x, coarse_along_z)
    strides = [pl.ds(j, SUBLANES, stride=vectors) for j in range(vectors)]

    def raw_plane(ref, *where):
        return tuple(ref[(*where, stride)] for stride in strides)

    def plane_of(ref, *where):
        return tuple(ref[(*where, j)] for j in range(ref.shape[-3]))

    def put(ref, plane, *where):
        for j, vector in enumerate(plane):
            ref[(*where, j)] = vector

    def prepare(ks):
        for k in ks:
            rate = raw_plane(rates, k)
            put(pull, each(lambda r: r * fine_center, rate), k)
            put(keep, each(lambda r: 1.0 - r, rate), k)

    def restricted(upper, lower):
        merged = each(jnp.add, upper, lower)
        averages = []
        for j in range(coarse_vectors):
            total = merged[2 * j] + merged[2 * j + 1]
            pair_sum = total + jnp.where(even, turned(total, -1, 1), turned(total, 1, 1))
            averages.append(pair_sum * 0.125)
        return tuple(averages)

    def raw_restricted(ref, k, *lead):
        return restricted(raw_plane(ref, *lead, 2 * k), raw_plane(ref, *lead, 2 * k + 1))

    def field_restricted(s, k):
        return restricted(plane_of(field, s, 2 * k), plane_of(field, s, 2 * k + 1))

    def coarse_rates(ks):
        weights = {k: raw_restricted(rates, k) for k in ks}
        return (
            {k: each(lambda v: v * coarse_center, w) for k, w in weights.items()},
            {k: each(lambda v: 1.0 - v, w) for k, w in weights.items()},
        )

    def stepped(trio, held, pulls, keeps, along):
        behind, middle, beyond = trio
        if middle is None and behind is not None and beyond is not None:
            deep = each(
                lambda b, f: blend(b, None, None, along) + blend(None, None, f, along), behind, beyond
            )
        else:
            there = [p for p in trio if p is not None]

            def mix(*given):
                given = iter(given)
                return blend(*(None if p is None else next(given) for p in trio), along)

            deep = each(mix, *there)
        if held is None:
            return each(jnp.multiply, pulls, deep)
        return each(lambda p, d, q, h: p * d + q * h, pulls, deep, keeps, held)

    def coarse_filtered(plane):
        return row_filtered(each(lambda v: lane_filtered(v, 2, coarse_along_y), plane), coarse_along_x)

    def advance(coarse, mixes, pulls, keeps, wanted):
        moved = [None] * coarse_layers
        for k in wanted:
            trio = mixes[k - 1], mixes[k], mixes[(k + 1) % coarse_layers]
            if any(p is not None for p in trio):
                moved[k] = stepped(trio, coarse[k], pulls[k], keeps[k], coarse_along_z)
        return moved

    def all_filtered(coarse):
        return [None if c is None else coarse_filtered(c) for c in coarse]

    def packed(coarse, shift=0):
        def layer(k):
            return coarse[(k + shift) % coarse_layers]

        return [each(lambda a, b: jnp.where(even, a, b), layer(k), layer(k + half)) for k in range(half)]

    def shifted(plane):
        return {n: each(lambda v: turned(v, n, 1), plane) for n in (1, 2, 3, -1, -2, -3)} | {0: plane}

    def mixed_lanes(t, even_by, odd_by):
        trio = [
            t[even_by + n]
            if even_by == odd_by
            else each(lambda a, b: jnp.where(even, a, b), t[even_by + n], t[odd_by + n])
            for n in (2, 0, -2)
        ]
        return trio[1], row_filtered(each(lambda *v: blend(*v, coarse_along_y), *trio), coarse_along_x)

    def advance_packed(coarse, pulls, keeps):
        turns = [shifted(c) for c in coarse]
        planes = [mixed_lanes(t, 0, 0)[1] for t in turns]
        low, high = mixed_lanes(turns[-1], -1, 1)[1], mixed_lanes(turns[0], -1, 1)[1]
        ring = [low] + planes + [high]
        return [
            stepped(ring[k : k + 3], coarse[k], pulls[k], keeps[k], coarse_along_z) for k in range(half)
        ]

    def advance_opened(coarse, pulls, keeps):
        turns = [shifted(c) for c in coarse]

        def opened(k):
            k = k % coarse_layers
            return mixed_lanes(turns[k % half], *((0, 1) if k < half else (-1, 0)))

        ring = [opened(k) for k in range(-1, coarse_depth + 1)]
        return [
            stepped([r[1] for r in ring[k : k + 3]], ring[k + 1][0], pulls[k], keeps[k], coarse_along_z)
            for k in range(coarse_depth)
        ]

    def open_lanes(coarse, k):
        both = coarse[k % half]
        if k < half:
            return each(lambda v: jnp.where(even, v, turned(v, 1, 1)), both)
        return each(lambda v: jnp.where(even, turned(v, -1, 1), v), both)

    def plus(first, second):
        return [
            b if a is None else a if b is None else each(jnp.add, a, b) for a, b in zip(first, second)
        ]

    def packed_in(ref, *where):
        return [plane_of(ref, *where, k) for k in range(half)]

    def grown(ks):
        return sorted({(k + n) % layers for k in ks for n in (-1, 0, 1)})

    def held_plane(s, turn, k):
        return raw_plane(state, s, k) if turn == 0 else plane_of(field, s, k)

    def spread(s, turn, ks):
        for k in ks:
            sides = each(lambda v: lane_filtered(v, 1, fine_along_y), held_plane(s, turn, k))
            put(mixed, row_filtered(sides, fine_along_x), turn % 2, s, k)

    def settle(s, turn, live, ks):
        for k in ks:
            trio = [
                plane_of(mixed, turn % 2, s, n % layers) if n % layers in live else None
                for n in (k - 1, k, k + 1)
            ]
            held = held_plane(s, turn, k) if k in live else None
            put(field, stepped(trio, held, plane_of(pull, k), plane_of(keep, k), fine_along_z), s, k)

    own_layers, own_coarse = list(range(depth)), list(range(coarse_depth))
    all_layers, all_coarse = list(range(layers)), list(range(coarse_layers))
    nothing = (jnp.zeros((SUBLANES, lanes), jnp.float32),) * coarse_vectors

    def each_fine(coarse, k):
        return tuple(coarse[k // 2][j // 2] for j in range(vectors))

    def sent_on(s, guess, ks):
        for k in ks:
            if guess[k // 2] is not None:
                put(field, each(jnp.subtract, plane_of(field, s, k), each_fine(guess, k)), s, k)

    def hand_in(ref, plane, k):
        for stride, vector in zip(strides, plane):
            ref[0, k, stride, :] = vector

    @pl.when(leads)
    def _():
        for j in range(2, groups):
            @pl.when(group - j >= 0)
            def _():
                signal(far_open, leader(group - j, 0))

        rate_load.wait()
        for i in others:
            rate_copy(i).start()
        state_load.wait()

        @pl.when(last)
        def _():
            for i in range(parts):
                next_copy(i).start()

        prepare(own_layers)
        lives = [own_layers]
        for _ in range(FINE):
            lives.append(grown(lives[-1]))
        ready_now = [own_layers]
        for turn in range(FINE):
            known = set(ready_now[-1])
            ready_now.append([
                k for k in own_layers
                if all(n % layers in known or n % layers not in lives[turn] for n in (k - 1, k, k + 1))
            ])

        def early(s):
            for turn in range(FINE):
                spread(s, turn, ready_now[turn])
                settle(s, turn, lives[turn], ready_now[turn + 1])

        def late(turn):
            for s in (0, 1):
                spread(s, turn, [k for k in lives[turn] if k not in ready_now[turn]])
            for s in (0, 1):
                settle(
                    s, turn, lives[turn], [k for k in lives[turn + 1] if k not in ready_now[turn + 1]]
                )

        def begin_of(s):
            begin = [raw_restricted(state, k, s) for k in own_coarse]
            begin += [None] * (coarse_layers - coarse_depth)
            return begin, all_filtered(begin)

        early(1)
        begins = {1: begin_of(1)}
        own_pulls, own_keeps = coarse_rates(own_coarse)
        pl.semaphore_wait(here, 1)

        @pl.when(group > 0)
        def _():
            signal(near_open, leader(group - 1, 0))

        raw_copy().wait_recv()
        early(0)
        begins[0] = begin_of(0)
        drain(arrive.at[1], rates.at[pl.ds(0, depth * (parts - 1))])
        for i in others:
            hand_copy(i).start()

        @pl.when(~last)
        def _():
            pl.semaphore_wait(near_open, 1)
            for i in others:
                signal(across, leader(group, i))
            next_copy(0).start()

        prepare([k for k in all_layers if k not in own_layers])
        for turn in range(FINE):
            late(turn)
        live = lives[-1]
        pulls, keeps = coarse_rates(all_coarse[coarse_depth:])
        pulls, keeps = own_pulls | pulls, own_keeps | keeps
        guesses = []
        for s, gate in ((0, jnp.where(group > 0, 1.0, 0.0)), (1, None)):
            guess = advance(*begins[s], pulls, keeps, all_coarse)
            if gate is not None:
                guess = [g if g is None else each(lambda v: gate * v, g) for g in guess]
            guesses.append(guess)
        for s in (0, 1):
            for k in all_layers:
                if k not in live:
                    put(field, (jnp.zeros((SUBLANES, lanes), jnp.float32),) * vectors, s, k)

        def term_of(s):
            terms = []
            for k in all_coarse:
                fine = field_restricted(s, k) if 2 * k in live else nothing
                guess = guesses[s][k]
                terms.append(fine if guess is None else each(jnp.subtract, fine, guess))
            return terms

        term, after = term_of(0), term_of(1)
        run = plus(advance(term, all_filtered(term), pulls, keeps, all_coarse), after)
        for i in range(parts):
            shift = i * coarse_depth
            for k, c in enumerate(packed(run, shift)):
                put(shares, c, i, 0, k)
            for k in own_coarse:
                put(crown, run[(k + shift) % coarse_layers], i, k)

        @pl.when(last)
        def _():
            for i in reversed(range(parts)):
                crown_copy(i).start()

        @pl.when(~last & (group > 0))
        def _():
            for i in reversed(range(parts)):
                wrap_copy(i).start()

        for i in others:
            share_copy(i, 0).start()
        for i in range(parts):
            for k, c in enumerate(packed(term, i * coarse_depth)):
                put(shares, c, i, 1, k)
        sent_on(1, guesses[1], all_layers)

        @pl.when(group + 2 < groups)
        def _():
            pl.semaphore_wait(far_open, groups - 2 - group)

        drain(arrive.at[3], shares_in.at[0])
        total = packed_in(shares, 0, 0)
        for r in others:
            total = plus(total, packed_in(shares_in, 0, r - 1))
        for k in range(half):
            put(sums, total[k], group, k)
        for j in reversed(range(1, groups)):
            @pl.when(group + j < groups)
            def _():
                sum_copy(j).start()

        @pl.when(~last)
        def _():
            if parts > 1:
                pl.semaphore_wait(across, parts - 1)
            for i in others:
                next_copy(i).start()

        @pl.when(group == 0)
        def _():
            first_copy().start()

        for i in others:
            share_copy(i, 1).start()

        packed_pulls, packed_keeps = packed(pulls), packed(keeps)

        def twice(coarse):
            for _ in range(2):
                coarse = advance_packed(coarse, packed_pulls, packed_keeps)
            return coarse

        @pl.when(group > 0)
        def _():
            drain(arrive.at[line], sums.at[0])

        for i in others:
            part_copy(i).start()

        @pl.when(group == 0)
        def _():
            for k in range(half):
                put(base, nothing, k)

        @pl.when(group > 0)
        def _():
            def pass_group(index, coarse):
                coarse = twice(coarse)
                drain(arrive.at[line + index], sums.at[index])
                return plus(coarse, packed_in(sums, index))

            coarse = lax.fori_loop(1, group, pass_group, packed_in(sums, 0))
            for k in range(half):
                put(base, coarse[k], k)

        coarse = packed_in(base)
        ahead = advance_opened(coarse, pulls, keeps)

        @pl.when(group > 0)
        def _():
            for k in own_coarse:
                put(heads, open_lanes(coarse, k), 0, k)
                put(heads, ahead[k], 1, k)
            head_copy().start()

        drain(arrive.at[6], shares_in.at[1])
        middle = packed_in(shares, 0, 1)
        for r in others:
            middle = plus(middle, packed_in(shares_in, 1, r - 1))
        finish = advance_opened(
            plus(advance_packed(coarse, packed_pulls, packed_keeps), middle), pulls, keeps
        )
        corr_copy().wait_recv()
        drain(arrive.at[4], parts_in)
        for k in own_layers:
            hand_in(next_ref, each(jnp.add, plane_of(corr_in, k), each_fine(ahead, k)), k)
            held = plane_of(field, 1, k)
            for r in others:
                held = each(jnp.add, held, plane_of(parts_in, r - 1, k))
            hand_in(end_ref, each(jnp.add, held, each_fine(finish, k)), k)
        away = pl.ds(0, depth * (parts - 1))
        drain(leave.at[0], rates.at[away])
        drain(leave.at[1], rates.at[away])
        drain(leave.at[2], state.at[1])
        drain(leave.at[4], shares_in.at[0])
        drain(leave.at[8], shares_in.at[1])
        drain(leave.at[5], parts_in)
        for j in range(1, groups):
            @pl.when(groups - 1 - group == j)
            def _():
                drain(leave.at[7], sums.at[pl.ds(0, j)])

        @pl.when(last)
        def _():
            drain(leave.at[3], crown_in)

        @pl.when(~last & (group > 0))
        def _():
            drain(leave.at[3], wraps.at[0])

        @pl.when(group == 0)
        def _():
            drain(leave.at[3], sums.at[0])

        @pl.when(group > 0)
        def _():
            drain(leave.at[6], heads)

    @pl.when(helps)
    def _():
        signal(here, leader(group, 0))
        state_load.wait()
        raw_copy().start()
        rate_load.wait()
        prepare(own_layers)
        raw_copy().wait_send()
        for i in others:
            side_copy(i).start()
        away = pl.ds(0, depth * (parts - 1))
        drain(arrive.at[2], rates.at[away])
        drain(arrive.at[1], rates.at[away])
        prepare([k for k in all_layers if k not in own_layers])
        pulls, keeps = coarse_rates(all_coarse)

        def solve(s, gate):
            begin = [raw_restricted(state, k, s) for k in all_coarse]
            guess = advance(begin, all_filtered(begin), pulls, keeps, own_coarse)
            if gate is not None:
                guess = [g if g is None else each(lambda v: gate * v, g) for g in guess]
            wanted = [own_layers]
            for _ in range(1, FINE):
                wanted.append(grown(wanted[-1]))
            for turn in range(FINE):
                reach = wanted[FINE - 1 - turn]
                spread(s, turn, grown(reach))
                settle(s, turn, all_layers, reach)
            sent_on(s, guess, own_layers)

        solve(0, jnp.where(group > 0, 1.0, 0.0))
        corr_copy().start()
        packed_pulls, packed_keeps = packed(pulls), packed(keeps)

        def arrived(index):
            drain(arrive.at[line + index], wraps.at[index])

        def with_arrived(coarse, index):
            for r in range(parts):
                coarse = plus(coarse, packed_in(wraps, index, r))
            return coarse

        def twice(coarse):
            for _ in range(2):
                coarse = advance_packed(coarse, packed_pulls, packed_keeps)
            return coarse

        def second_solve():
            solve(1, None)
            before = [field_restricted(1, k) for k in own_coarse]
            sent_on(1, before, own_layers)

        @pl.when(group == 0)
        def _():
            for k in own_layers:
                hand_in(end_ref, plane_of(field, 0, k), k)
            drain(arrive.at[line], wraps.at[0, 0])
            coarse = twice(packed_in(wraps, 0, 0))
            midway = max(groups - 3, 1)
            for index in range(1, midway):
                arrived(index)
            drain(arrive.at[0], state.at[1])
            for index in range(1, midway):
                coarse = twice(with_arrived(coarse, index))
            second_solve()
            for index in range(midway, groups - 1):
                arrived(index)
                coarse = with_arrived(coarse, index)
                if index < groups - 2:
                    coarse = twice(coarse)
            coarse = advance_packed(coarse, packed_pulls, packed_keeps)
            coarse = advance_opened(coarse, pulls, keeps)
            for k in own_layers:
                put(field, each(jnp.add, plane_of(field, 1, k), each_fine(coarse, k)), 1, k)
            drain(arrive.at[line + groups - 1], crown_in)
            for k in own_layers:
                following = plane_of(field, 1, k)
                for r in range(parts):
                    offset = each_fine([plane_of(crown_in, r, c) for c in own_coarse], k)
                    following = each(jnp.add, following, offset)
                hand_in(next_ref, following, k)

        @pl.when(group > 0)
        def _():
            drain(arrive.at[0], state.at[1])
            second_solve()
            head_copy().wait_recv()
            for k in own_layers:
                coarse, ahead = ([plane_of(heads_in, n, c) for c in own_coarse] for n in range(2))
                hand_in(next_ref, each(jnp.add, plane_of(field, 1, k), each_fine(coarse, k)), k)
                hand_in(end_ref, each(jnp.add, plane_of(field, 0, k), each_fine(ahead, k)), k)

        drain(leave.at[2], corr_in)
        drain(leave.at[1], rates.at[away])


def hand_out_kernel(end_ref, next_ref, end_out, next_out, sems):
    copies = [
        pltpu.make_async_copy(end_ref, end_out, sems.at[0]),
        pltpu.make_async_copy(next_ref, next_out, sems.at[1]),
    ]
    for copy in copies:
        copy.start()
    for copy in copies:
        copy.wait()


def hand_out(end, following):
    return pl.pallas_call(
        hand_out_kernel,
        out_shape=[jax.ShapeDtypeStruct(end.shape, end.dtype)] * 2,
        in_specs=[pl.BlockSpec(memory_space=pltpu.VMEM)] * 2,
        out_specs=[pl.BlockSpec(memory_space=pl.ANY)] * 2,
        scratch_shapes=[pltpu.SemaphoreType.DMA((2,))],
    )(*(pltpu.with_memory_space_constraint(x, pltpu.VMEM) for x in (end, following)))


def solution(mesh):
    slabs, parts = mesh.shape["tm"], mesh.shape["gz"]

    def per_device(starts, cell_rates):
        depth, rows, lanes = cell_rates.shape
        layers = depth * parts
        groups = slabs // 2
        vectors = rows // SUBLANES
        fine = (vectors, SUBLANES, lanes)
        coarse = (vectors // 2, SUBLANES, lanes)
        packed = (layers // 4, *coarse)
        lead = (depth // 2, *coarse)
        aside = max(parts - 1, 1)
        dma = pltpu.SemaphoreType.DMA

        def vmem(*shape):
            return pltpu.VMEM(shape, jnp.float32)

        ends = pl.pallas_call(
            functools.partial(kernel, slabs, parts),
            out_shape=[pltpu.VMEM(starts.shape, jnp.float32)] * 2,
            in_specs=[pl.BlockSpec(memory_space=pl.ANY)] * 2,
            out_specs=[pl.BlockSpec(memory_space=pltpu.VMEM)] * 2,
            scratch_shapes=[
                vmem(2, layers, rows, lanes),
                vmem(layers, rows, lanes),
                vmem(layers, *fine),
                vmem(layers, *fine),
                vmem(2, 2, layers, *fine),
                vmem(2, layers, *fine),
                vmem(parts, 2, *packed),
                vmem(2, aside, *packed),
                vmem(groups, *packed),
                vmem(groups, parts, *packed),
                vmem(parts, *lead),
                vmem(parts, *lead),
                vmem(2, *lead),
                vmem(2, *lead),
                vmem(depth, *fine),
                vmem(aside, depth, *fine),
                vmem(*packed),
                pltpu.SemaphoreType.REGULAR((4,)),
                dma((9,)),
                dma((7 + groups,)),
            ],
            compiler_params=pltpu.CompilerParams(collective_id=0, has_side_effects=True),
        )(starts, cell_rates)
        return hand_out(*ends)

    return jax.shard_map(
        per_device,
        mesh=mesh,
        in_specs=(P("tm", "gz", None, None), P("gz", None, None)),
        out_specs=(P("tm", "gz", None, None), P("tm", "gz", None, None)),
        check_vma=False,
    )
```

time: 14.4 us -> 13.7 us (0.951)
  Pallas kernels: 13.6 us -> 12.9 us
    pallas_call x1, Pallas kernels: 12.9 us -> 12.2 us  [per_device(): pl.pallas_call(functools.partial(kernel, slabs, parts), out_shape=[pltpu....]
where the time goes in v3:
time: 13.7 us; the launch traced here: 13.6 us
  Pallas kernels  12.9 us (94%)
  between operations  0.64 us (5%)
    pallas_call x1, Pallas kernels, per_device(): pl.pallas_call(functools.partial(kernel, slabs, parts), out_shape=[pltpu....  12.2 us
    pallas_call x1, Pallas kernels, hand_out(): pl.pallas_call(hand_out_kernel, out_shape=[jax.ShapeDtypeStruct(end.shape...  0.67 us

profile of v3, /device:TPU:0, one launch (start us, length us, event | category | flops | bytes accessed | tf_op | source)
XLA Modules:
  0.0 13.6 jit_solution(9843564304070761793)
XLA Ops:
  0.6 12.2 %shard_map.41 = (f32[1,4,32,128]{3,2,1,0:T(8,128)S(1)}, f32[1,4,32,128]{3,2,1,0:T(8,128)S(1)}) custom-call(f32[1,4,32,128]{3,2,1,0:T(8,128)} %starts_ref.1, f32[4,32,128]{2,1,0:T(8,128)} %rates_ref.1), custom_call_target="tpu_custom_call" | custom-call | tf_op jit(solution)/shard_map/pallas_call | solution.py:727
  12.9 0.7 %shard_map.42 = (f32[1,4,32,128]{3,2,1,0:T(8,128)}, f32[1,4,32,128]{3,2,1,0:T(8,128)}) custom-call(f32[1,4,32,128]{3,2,1,0:T(8,128)S(1)} %get-tuple-element.4.end_ref, f32[1,4,32,128]{3,2,1,0:T(8,128)S(1)} %get-tuple-element.5.next_ref), custom_call_target="tpu_custom_call" | custom-call | tf_op jit(solution)/shard_map/pallas_call | solution.py:700

commit v4 on v3

--- a/solution.py
+++ b/solution.py
@@ -59,7 +59,7 @@
 def kernel(
     slabs, parts, starts_ref, rates_ref, end_ref, next_ref,
     state, rates, pull, keep, mixed, field, shares, shares_in, sums, wraps, crown, crown_in,
-    heads, heads_in, corr_in, parts_in, base,
+    heads, heads_in, corr_in, parts_in, base, raw_in,
     ready, leave, arrive,
 ):
     depth, rows, lanes = rates_ref.shape
@@ -73,6 +73,7 @@
     group, place = me // 2, lax.rem(me, 2)
     leads, helps = place == 1, place == 0
     last = group == groups - 1
+    direct, proxy = (group == 0) & (part == 0), (group == 0) & (part > 0)
 
     def block(r):
         return pl.ds(r % parts * depth, depth)
@@ -101,7 +102,7 @@
     others = range(1, parts)
     barrier = pltpu.get_barrier_semaphore()
     here, near_open, far_open, across = (ready.at[n] for n in range(4))
-    line = 7
+    line = 8
 
     @pl.when(leads)
     def _():
@@ -113,18 +114,24 @@
             def _():
                 signal(barrier, leader(group + j, 0))
 
+        @pl.when(proxy)
+        def _():
+            for j in range(1, groups):
+                for i in others:
+                    signal(barrier, leader(j, i))
+
     @pl.when(helps)
     def _():
         for i in others:
             signal(barrier, helper(group, i))
 
-        @pl.when(group == 0)
+        @pl.when(direct)
         def _():
             for j in range(1, groups):
                 for i in range(parts):
                     signal(barrier, leader(j, i))
 
-    earlier = group + jnp.where(group > 0, parts, 0)
+    earlier = group + jnp.where(group > 0, parts - jnp.where(part > 0, 1, 0), 0)
     pl.semaphore_wait(barrier, jnp.where(leads, parts - 1 + earlier, parts))
 
     def drain(sem, ref):
@@ -149,16 +156,30 @@
             state.at[0, own], state.at[0, block(parts - i)], leave.at[1], arrive.at[2], helper(group, i)
         )
 
+    def offset_to(q):
+        return lax.rem(q + parts - part, parts)
+
+    def home(i):
+        q = lax.rem(part + i, parts)
+        return {"tm": jnp.where(q == 0, 0, 1), "gz": q}
+
+    def raw_next(i, send_sem, peer):
+        r = lax.rem(parts - i, parts)
+        return remote(state.at[1, own], raw_in.at[pl.ds(r * depth, depth)], send_sem, arrive.at[7], peer)
+
     def next_copy(i):
-        return remote(
-            state.at[1, own], state.at[1, block(parts - i)], leave.at[2], arrive.at[0],
-            helper(lax.rem(group + 1, groups), i),
-        )
+        return raw_next(i, leave.at[2], helper(group + 1, i))
+
+    def round_copy(i):
+        return raw_next(i, leave.at[2], home(i))
+
+    def forward_copy():
+        return remote(raw_in, raw_in, leave.at[3], arrive.at[7], helper(0, 0))
 
     def wrap_copy(i):
         return remote(
-            shares.at[i, 0], wraps.at[group, (parts - i) % parts], leave.at[3], arrive.at[line + group],
-            helper(0, i),
+            shares.at[i, 0], wraps.at[group, lax.rem(parts - i, parts)], leave.at[3], arrive.at[line + group],
+            home(i),
         )
 
     def first_copy():
@@ -166,8 +187,8 @@
 
     def crown_copy(i):
         return remote(
-            crown.at[i], crown_in.at[(parts - i) % parts], leave.at[3], arrive.at[line + group],
-            helper(0, i),
+            crown.at[i], crown_in.at[lax.rem(parts - i, parts)], leave.at[3], arrive.at[line + group],
+            home(i),
         )
 
     def share_copy(i, n):
@@ -221,6 +242,21 @@
             averages.append(pair_sum * 0.125)
         return tuple(averages)
 
+    def restricted_and_filtered(upper, lower, guess):
+        merged = each(jnp.add, upper, lower)
+        total = tuple(merged[2 * j] + merged[2 * j + 1] for j in range(coarse_vectors))
+        if guess is not None:
+            total = each(lambda t, g: t - 4.0 * g, total, guess)
+        total = each(lambda t: t * 0.125, total)
+        t = shifted(total)
+
+        def pair(n):
+            return each(lambda here, a, b: here + jnp.where(even, a, b), t[n], t[n - 1], t[n + 1])
+
+        here = pair(0)
+        sides = each(lambda *v: blend(*v, coarse_along_y), pair(2), here, pair(-2))
+        return here, row_filtered(sides, coarse_along_x)
+
     def raw_restricted(ref, k, *lead):
         return restricted(raw_plane(ref, *lead, 2 * k), raw_plane(ref, *lead, 2 * k + 1))
 
@@ -323,21 +359,24 @@
     def grown(ks):
         return sorted({(k + n) % layers for k in ks for n in (-1, 0, 1)})
 
-    def held_plane(s, turn, k):
-        return raw_plane(state, s, k) if turn == 0 else plane_of(field, s, k)
-
-    def spread(s, turn, ks):
+    def origin(s, k):
+        return raw_plane(state, s, k)
+
+    def held_plane(s, turn, k, first):
+        return first(s, k) if turn == 0 else plane_of(field, s, k)
+
+    def spread(s, turn, ks, first=origin):
         for k in ks:
-            sides = each(lambda v: lane_filtered(v, 1, fine_along_y), held_plane(s, turn, k))
+            sides = each(lambda v: lane_filtered(v, 1, fine_along_y), held_plane(s, turn, k, first))
             put(mixed, row_filtered(sides, fine_along_x), turn % 2, s, k)
 
-    def settle(s, turn, live, ks):
+    def settle(s, turn, live, ks, first=origin):
         for k in ks:
             trio = [
                 plane_of(mixed, turn % 2, s, n % layers) if n % layers in live else None
                 for n in (k - 1, k, k + 1)
             ]
-            held = held_plane(s, turn, k) if k in live else None
+            held = held_plane(s, turn, k, first) if k in live else None
             put(field, stepped(trio, held, plane_of(pull, k), plane_of(keep, k), fine_along_z), s, k)
 
     own_layers, own_coarse = list(range(depth)), list(range(coarse_depth))
@@ -370,8 +409,8 @@
 
         @pl.when(last)
         def _():
-            for i in range(parts):
-                next_copy(i).start()
+            for q in range(parts):
+                round_copy(offset_to(q)).start()
 
         prepare(own_layers)
         lives = [own_layers]
@@ -443,16 +482,24 @@
                 if k not in live:
                     put(field, (jnp.zeros((SUBLANES, lanes), jnp.float32),) * vectors, s, k)
 
-        def term_of(s):
-            terms = []
-            for k in all_coarse:
-                fine = field_restricted(s, k) if 2 * k in live else nothing
-                guess = guesses[s][k]
-                terms.append(fine if guess is None else each(jnp.subtract, fine, guess))
-            return terms
-
-        term, after = term_of(0), term_of(1)
-        run = plus(advance(term, all_filtered(term), pulls, keeps, all_coarse), after)
+        def fine_of(s, k):
+            return plane_of(field, s, 2 * k), plane_of(field, s, 2 * k + 1)
+
+        def zero_guess(s, k):
+            return guesses[s][k] if guesses[s][k] is not None else nothing
+
+        both = [
+            restricted_and_filtered(*fine_of(0, k), guesses[0][k])
+            if 2 * k in live
+            else (each(jnp.negative, zero_guess(0, k)), coarse_filtered(each(jnp.negative, zero_guess(0, k))))
+            for k in all_coarse
+        ]
+        term = [b[0] for b in both]
+        after = [
+            each(jnp.subtract, restricted(*fine_of(1, k)) if 2 * k in live else nothing, zero_guess(1, k))
+            for k in all_coarse
+        ]
+        run = plus(advance(term, [b[1] for b in both], pulls, keeps, all_coarse), after)
         for i in range(parts):
             shift = i * coarse_depth
             for k, c in enumerate(packed(run, shift)):
@@ -462,13 +509,13 @@
 
         @pl.when(last)
         def _():
-            for i in reversed(range(parts)):
-                crown_copy(i).start()
+            for q in range(parts):
+                crown_copy(offset_to(q)).start()
 
         @pl.when(~last & (group > 0))
         def _():
-            for i in reversed(range(parts)):
-                wrap_copy(i).start()
+            for q in range(parts):
+                wrap_copy(offset_to(q)).start()
 
         for i in others:
             share_copy(i, 0).start()
@@ -476,6 +523,12 @@
             for k, c in enumerate(packed(term, i * coarse_depth)):
                 put(shares, c, i, 1, k)
         sent_on(1, guesses[1], all_layers)
+
+        @pl.when(group == 0)
+        def _():
+            for i in others:
+                part_copy(i).start()
+                share_copy(i, 1).start()
 
         @pl.when(group + 2 < groups)
         def _():
@@ -499,12 +552,14 @@
             for i in others:
                 next_copy(i).start()
 
-        @pl.when(group == 0)
+        @pl.when(direct)
         def _():
             first_copy().start()
 
-        for i in others:
-            share_copy(i, 1).start()
+        @pl.when(group > 0)
+        def _():
+            for i in others:
+                share_copy(i, 1).start()
 
         packed_pulls, packed_keeps = packed(pulls), packed(keeps)
 
@@ -516,9 +571,8 @@
         @pl.when(group > 0)
         def _():
             drain(arrive.at[line], sums.at[0])
-
-        for i in others:
-            part_copy(i).start()
+            for i in others:
+                part_copy(i).start()
 
         @pl.when(group == 0)
         def _():
@@ -564,7 +618,7 @@
         away = pl.ds(0, depth * (parts - 1))
         drain(leave.at[0], rates.at[away])
         drain(leave.at[1], rates.at[away])
-        drain(leave.at[2], state.at[1])
+        drain(leave.at[2], raw_in)
         drain(leave.at[4], shares_in.at[0])
         drain(leave.at[8], shares_in.at[1])
         drain(leave.at[5], parts_in)
@@ -581,11 +635,36 @@
         def _():
             drain(leave.at[3], wraps.at[0])
 
-        @pl.when(group == 0)
+        @pl.when(direct)
         def _():
             drain(leave.at[3], sums.at[0])
 
-        @pl.when(group > 0)
+        @pl.when(proxy)
+        def _():
+            drain(arrive.at[7], raw_in)
+            forward_copy().start()
+
+            def pass_group(index, coarse):
+                coarse = twice(coarse)
+                drain(arrive.at[line + index], wraps.at[index])
+                for r in range(parts):
+                    coarse = plus(coarse, packed_in(wraps, index, r))
+                return coarse
+
+            coarse = lax.fori_loop(1, groups - 1, pass_group, packed_in(sums, 0))
+            coarse = advance_packed(coarse, packed_pulls, packed_keeps)
+            coarse = advance_opened(coarse, pulls, keeps)
+            drain(arrive.at[line + groups - 1], crown_in)
+            for k in own_coarse:
+                following = coarse[k]
+                for r in range(parts):
+                    following = each(jnp.add, following, plane_of(crown_in, r, k))
+                put(heads, following, 0, k)
+                put(heads, nothing, 1, k)
+            head_copy().start()
+            drain(leave.at[3], raw_in)
+
+        @pl.when(~direct)
         def _():
             drain(leave.at[6], heads)
 
@@ -606,7 +685,10 @@
         pulls, keeps = coarse_rates(all_coarse)
 
         def solve(s, gate):
-            begin = [raw_restricted(state, k, s) for k in all_coarse]
+            def first(s, k):
+                return raw_plane(state, 0, k) if s == 0 else raw_plane(raw_in, k)
+
+            begin = [restricted(first(s, 2 * k), first(s, 2 * k + 1)) for k in all_coarse]
             guess = advance(begin, all_filtered(begin), pulls, keeps, own_coarse)
             if gate is not None:
                 guess = [g if g is None else each(lambda v: gate * v, g) for g in guess]
@@ -615,8 +697,8 @@
                 wanted.append(grown(wanted[-1]))
             for turn in range(FINE):
                 reach = wanted[FINE - 1 - turn]
-                spread(s, turn, grown(reach))
-                settle(s, turn, all_layers, reach)
+                spread(s, turn, grown(reach), first)
+                settle(s, turn, all_layers, reach, first)
             sent_on(s, guess, own_layers)
 
         solve(0, jnp.where(group > 0, 1.0, 0.0))
@@ -641,7 +723,7 @@
             before = [field_restricted(1, k) for k in own_coarse]
             sent_on(1, before, own_layers)
 
-        @pl.when(group == 0)
+        @pl.when(direct)
         def _():
             for k in own_layers:
                 hand_in(end_ref, plane_of(field, 0, k), k)
@@ -650,7 +732,7 @@
             midway = max(groups - 3, 1)
             for index in range(1, midway):
                 arrived(index)
-            drain(arrive.at[0], state.at[1])
+            drain(arrive.at[7], raw_in)
             for index in range(1, midway):
                 coarse = twice(with_arrived(coarse, index))
             second_solve()
@@ -671,9 +753,9 @@
                     following = each(jnp.add, following, offset)
                 hand_in(next_ref, following, k)
 
-        @pl.when(group > 0)
-        def _():
-            drain(arrive.at[0], state.at[1])
+        @pl.when(~direct)
+        def _():
+            drain(arrive.at[7], raw_in)
             second_solve()
             head_copy().wait_recv()
             for k in own_layers:
@@ -747,9 +829,10 @@
                 vmem(depth, *fine),
                 vmem(aside, depth, *fine),
                 vmem(*packed),
+                vmem(layers, rows, lanes),
                 pltpu.SemaphoreType.REGULAR((4,)),
                 dma((9,)),
-                dma((7 + groups,)),
+                dma((8 + groups,)),
             ],
             compiler_params=pltpu.CompilerParams(collective_id=0, has_side_effects=True),
         )(starts, cell_rates)

time: 13.7 us -> 13.4 us (0.978)
  Pallas kernels: 12.9 us -> 12.6 us
    pallas_call x1, Pallas kernels: 12.2 us -> 11.9 us  [per_device(): pl.pallas_call(functools.partial(kernel, slabs, parts), out_shape=[pltpu....]
where the time goes in v4:
time: 13.4 us; the launch traced here: 13.2 us
  Pallas kernels  12.6 us (94%)
  between operations  0.64 us (5%)
    pallas_call x1, Pallas kernels, per_device(): pl.pallas_call(functools.partial(kernel, slabs, parts), out_shape=[pltpu....  11.9 us
    pallas_call x1, Pallas kernels, hand_out(): pl.pallas_call(hand_out_kernel, out_shape=[jax.ShapeDtypeStruct(end.shape...  0.67 us

profile of v4, /device:TPU:0, one launch (start us, length us, event | category | flops | bytes accessed | tf_op | source)
XLA Modules:
  0.0 13.2 jit_solution(18032851234568546600)
XLA Ops:
  0.6 11.9 %shard_map.41 = (f32[1,4,32,128]{3,2,1,0:T(8,128)S(1)}, f32[1,4,32,128]{3,2,1,0:T(8,128)S(1)}) custom-call(f32[1,4,32,128]{3,2,1,0:T(8,128)} %starts_ref.1, f32[4,32,128]{2,1,0:T(8,128)} %rates_ref.1), custom_call_target="tpu_custom_call" | custom-call | tf_op jit(solution)/shard_map/pallas_call | solution.py:809
  12.6 0.7 %shard_map.42 = (f32[1,4,32,128]{3,2,1,0:T(8,128)}, f32[1,4,32,128]{3,2,1,0:T(8,128)}) custom-call(f32[1,4,32,128]{3,2,1,0:T(8,128)S(1)} %get-tuple-element.4.end_ref, f32[1,4,32,128]{3,2,1,0:T(8,128)S(1)} %get-tuple-element.5.next_ref), custom_call_target="tpu_custom_call" | custom-call | tf_op jit(solution)/shard_map/pallas_call | solution.py:782

commit v5 on v4

--- a/solution.py
+++ b/solution.py
@@ -101,7 +101,7 @@
 
     others = range(1, parts)
     barrier = pltpu.get_barrier_semaphore()
-    here, near_open, far_open, across = (ready.at[n] for n in range(4))
+    here, near_open, far_open = (ready.at[n] for n in range(3))
     line = 8
 
     @pl.when(leads)
@@ -167,8 +167,11 @@
         r = lax.rem(parts - i, parts)
         return remote(state.at[1, own], raw_in.at[pl.ds(r * depth, depth)], send_sem, arrive.at[7], peer)
 
-    def next_copy(i):
-        return raw_next(i, leave.at[2], helper(group + 1, i))
+    def next_copy():
+        return raw_next(0, leave.at[2], helper(group + 1, 0))
+
+    def across_copy(i):
+        return remote(raw_in.at[own], raw_in.at[block(parts - i)], leave.at[3], arrive.at[0], helper(group, i))
 
     def round_copy(i):
         return raw_next(i, leave.at[2], home(i))
@@ -461,9 +464,7 @@
         @pl.when(~last)
         def _():
             pl.semaphore_wait(near_open, 1)
-            for i in others:
-                signal(across, leader(group, i))
-            next_copy(0).start()
+            next_copy().start()
 
         prepare([k for k in all_layers if k not in own_layers])
         for turn in range(FINE):
@@ -545,13 +546,6 @@
             def _():
                 sum_copy(j).start()
 
-        @pl.when(~last)
-        def _():
-            if parts > 1:
-                pl.semaphore_wait(across, parts - 1)
-            for i in others:
-                next_copy(i).start()
-
         @pl.when(direct)
         def _():
             first_copy().start()
@@ -618,7 +612,10 @@
         away = pl.ds(0, depth * (parts - 1))
         drain(leave.at[0], rates.at[away])
         drain(leave.at[1], rates.at[away])
-        drain(leave.at[2], raw_in)
+        @pl.when(~last)
+        def _():
+            drain(leave.at[2], raw_in.at[own])
+
         drain(leave.at[4], shares_in.at[0])
         drain(leave.at[8], shares_in.at[1])
         drain(leave.at[5], parts_in)
@@ -629,6 +626,7 @@
 
         @pl.when(last)
         def _():
+            drain(leave.at[2], raw_in)
             drain(leave.at[3], crown_in)
 
         @pl.when(~last & (group > 0))
@@ -729,14 +727,9 @@
                 hand_in(end_ref, plane_of(field, 0, k), k)
             drain(arrive.at[line], wraps.at[0, 0])
             coarse = twice(packed_in(wraps, 0, 0))
-            midway = max(groups - 3, 1)
-            for index in range(1, midway):
-                arrived(index)
             drain(arrive.at[7], raw_in)
-            for index in range(1, midway):
-                coarse = twice(with_arrived(coarse, index))
             second_solve()
-            for index in range(midway, groups - 1):
+            for index in range(1, groups - 1):
                 arrived(index)
                 coarse = with_arrived(coarse, index)
                 if index < groups - 2:
@@ -753,15 +746,29 @@
                     following = each(jnp.add, following, offset)
                 hand_in(next_ref, following, k)
 
+        @pl.when(proxy)
+        def _():
+            drain(arrive.at[7], raw_in)
+
+        @pl.when(group > 0)
+        def _():
+            drain(arrive.at[7], raw_in.at[own])
+            for i in others:
+                across_copy(i).start()
+            drain(arrive.at[0], raw_in.at[away])
+
         @pl.when(~direct)
         def _():
-            drain(arrive.at[7], raw_in)
             second_solve()
             head_copy().wait_recv()
             for k in own_layers:
                 coarse, ahead = ([plane_of(heads_in, n, c) for c in own_coarse] for n in range(2))
                 hand_in(next_ref, each(jnp.add, plane_of(field, 1, k), each_fine(coarse, k)), k)
                 hand_in(end_ref, each(jnp.add, plane_of(field, 0, k), each_fine(ahead, k)), k)
+
+        @pl.when(group > 0)
+        def _():
+            drain(leave.at[3], raw_in.at[away])
 
         drain(leave.at[2], corr_in)
         drain(leave.at[1], rates.at[away])
@@ -830,7 +837,7 @@
                 vmem(aside, depth, *fine),
                 vmem(*packed),
                 vmem(layers, rows, lanes),
-                pltpu.SemaphoreType.REGULAR((4,)),
+                pltpu.SemaphoreType.REGULAR((3,)),
                 dma((9,)),
                 dma((8 + groups,)),
             ],

time: 13.4 us -> 13.3 us (level)
  no operation moved by 1% of the time
where the time goes in v5:
time: 13.3 us; the launch traced here: 13.1 us
  Pallas kernels  12.5 us (94%)
  between operations  0.64 us (5%)
    pallas_call x1, Pallas kernels, per_device(): pl.pallas_call(functools.partial(kernel, slabs, parts), out_shape=[pltpu....  11.8 us
    pallas_call x1, Pallas kernels, hand_out(): pl.pallas_call(hand_out_kernel, out_shape=[jax.ShapeDtypeStruct(end.shape...  0.67 us

profile of v5, /device:TPU:0, one launch (start us, length us, event | category | flops | bytes accessed | tf_op | source)
XLA Modules:
  0.0 13.1 jit_solution(17236714604397018626)
XLA Ops:
  0.6 11.8 %shard_map.41 = (f32[1,4,32,128]{3,2,1,0:T(8,128)S(1)}, f32[1,4,32,128]{3,2,1,0:T(8,128)S(1)}) custom-call(f32[1,4,32,128]{3,2,1,0:T(8,128)} %starts_ref.1, f32[4,32,128]{2,1,0:T(8,128)} %rates_ref.1), custom_call_target="tpu_custom_call" | custom-call | tf_op jit(solution)/shard_map/pallas_call | solution.py:816
  12.5 0.7 %shard_map.42 = (f32[1,4,32,128]{3,2,1,0:T(8,128)}, f32[1,4,32,128]{3,2,1,0:T(8,128)}) custom-call(f32[1,4,32,128]{3,2,1,0:T(8,128)S(1)} %get-tuple-element.4.end_ref, f32[1,4,32,128]{3,2,1,0:T(8,128)S(1)} %get-tuple-element.5.next_ref), custom_call_target="tpu_custom_call" | custom-call | tf_op jit(solution)/shard_map/pallas_call | solution.py:789

commit v6 on v5

--- a/solution.py
+++ b/solution.py
@@ -81,9 +81,6 @@
     own = block(0)
     rate_load = pltpu.make_async_copy(rates_ref, rates.at[own], leave.at[5])
     state_load = pltpu.make_async_copy(starts_ref.at[0], state.at[place, own], leave.at[6])
-    rate_load.start()
-    state_load.start()
-
     def leader(g, i):
         return {"tm": 2 * g + 1, "gz": lax.rem(part + i, parts)}
 
@@ -108,6 +105,8 @@
     def _():
         for i in others:
             signal(barrier, leader(group, i))
+        rate_load.start()
+        state_load.start()
         signal(barrier, helper(group, 0))
         for j in range(1, groups):
             @pl.when(group + j < groups)
@@ -122,6 +121,8 @@
 
     @pl.when(helps)
     def _():
+        state_load.start()
+        rate_load.start()
         for i in others:
             signal(barrier, helper(group, i))
 
@@ -726,9 +727,13 @@
             for k in own_layers:
                 hand_in(end_ref, plane_of(field, 0, k), k)
             drain(arrive.at[line], wraps.at[0, 0])
-            coarse = twice(packed_in(wraps, 0, 0))
+            coarse = packed_in(wraps, 0, 0)
+            if groups > 2:
+                coarse = twice(coarse)
             drain(arrive.at[7], raw_in)
             second_solve()
+            drain(leave.at[2], corr_in)
+            drain(leave.at[1], rates.at[away])
             for index in range(1, groups - 1):
                 arrived(index)
                 coarse = with_arrived(coarse, index)
@@ -760,18 +765,18 @@
         @pl.when(~direct)
         def _():
             second_solve()
+            drain(leave.at[2], corr_in)
+            drain(leave.at[1], rates.at[away])
+
+            @pl.when(group > 0)
+            def _():
+                drain(leave.at[3], raw_in.at[away])
+
             head_copy().wait_recv()
             for k in own_layers:
                 coarse, ahead = ([plane_of(heads_in, n, c) for c in own_coarse] for n in range(2))
                 hand_in(next_ref, each(jnp.add, plane_of(field, 1, k), each_fine(coarse, k)), k)
                 hand_in(end_ref, each(jnp.add, plane_of(field, 0, k), each_fine(ahead, k)), k)
-
-        @pl.when(group > 0)
-        def _():
-            drain(leave.at[3], raw_in.at[away])
-
-        drain(leave.at[2], corr_in)
-        drain(leave.at[1], rates.at[away])
 
 
 def hand_out_kernel(end_ref, next_ref, end_out, next_out, sems):

time: 13.3 us -> 13.3 us (level)
  no operation moved by 1% of the time
where the time goes in v6:
time: 13.3 us; the launch traced here: 13.1 us
  Pallas kernels  12.5 us (94%)
  between operations  0.64 us (5%)
    pallas_call x1, Pallas kernels, per_device(): pl.pallas_call(functools.partial(kernel, slabs, parts), out_shape=[pltpu....  11.8 us
    pallas_call x1, Pallas kernels, hand_out(): pl.pallas_call(hand_out_kernel, out_shape=[jax.ShapeDtypeStruct(end.shape...  0.67 us

profile of v6, /device:TPU:0, one launch (start us, length us, event | category | flops | bytes accessed | tf_op | source)
XLA Modules:
  0.0 13.1 jit_solution(395361381335036115)
XLA Ops:
  0.6 11.8 %shard_map.41 = (f32[1,4,32,128]{3,2,1,0:T(8,128)S(1)}, f32[1,4,32,128]{3,2,1,0:T(8,128)S(1)}) custom-call(f32[1,4,32,128]{3,2,1,0:T(8,128)} %starts_ref.1, f32[4,32,128]{2,1,0:T(8,128)} %rates_ref.1), custom_call_target="tpu_custom_call" | custom-call | tf_op jit(solution)/shard_map/pallas_call | solution.py:821
  12.5 0.7 %shard_map.42 = (f32[1,4,32,128]{3,2,1,0:T(8,128)}, f32[1,4,32,128]{3,2,1,0:T(8,128)}) custom-call(f32[1,4,32,128]{3,2,1,0:T(8,128)S(1)} %get-tuple-element.4.end_ref, f32[1,4,32,128]{3,2,1,0:T(8,128)S(1)} %get-tuple-element.5.next_ref), custom_call_target="tpu_custom_call" | custom-call | tf_op jit(solution)/shard_map/pallas_call | solution.py:794

commit v7 on v6

--- a/solution.py
+++ b/solution.py
@@ -519,8 +519,11 @@
             for q in range(parts):
                 wrap_copy(offset_to(q)).start()
 
-        for i in others:
-            share_copy(i, 0).start()
+        @pl.when(~last)
+        def _():
+            for i in others:
+                share_copy(i, 0).start()
+
         for i in range(parts):
             for k, c in enumerate(packed(term, i * coarse_depth)):
                 put(shares, c, i, 1, k)
@@ -536,12 +539,15 @@
         def _():
             pl.semaphore_wait(far_open, groups - 2 - group)
 
-        drain(arrive.at[3], shares_in.at[0])
-        total = packed_in(shares, 0, 0)
-        for r in others:
-            total = plus(total, packed_in(shares_in, 0, r - 1))
-        for k in range(half):
-            put(sums, total[k], group, k)
+        @pl.when(~last)
+        def _():
+            drain(arrive.at[3], shares_in.at[0])
+            total = packed_in(shares, 0, 0)
+            for r in others:
+                total = plus(total, packed_in(shares_in, 0, r - 1))
+            for k in range(half):
+                put(sums, total[k], group, k)
+
         for j in reversed(range(1, groups)):
             @pl.when(group + j < groups)
             def _():
@@ -617,7 +623,10 @@
         def _():
             drain(leave.at[2], raw_in.at[own])
 
-        drain(leave.at[4], shares_in.at[0])
+        @pl.when(~last)
+        def _():
+            drain(leave.at[4], shares_in.at[0])
+
         drain(leave.at[8], shares_in.at[1])
         drain(leave.at[5], parts_in)
         for j in range(1, groups):

time: 13.3 us -> 13.3 us (level)
  no operation moved by 1% of the time
where the time goes in v7:
time: 13.3 us; the launch traced here: 13.1 us
  Pallas kernels  12.5 us (94%)
  between operations  0.64 us (5%)
    pallas_call x1, Pallas kernels, per_device(): pl.pallas_call(functools.partial(kernel, slabs, parts), out_shape=[pltpu....  11.8 us
    pallas_call x1, Pallas kernels, hand_out(): pl.pallas_call(hand_out_kernel, out_shape=[jax.ShapeDtypeStruct(end.shape...  0.67 us

profile of v7, /device:TPU:0, one launch (start us, length us, event | category | flops | bytes accessed | tf_op | source)
XLA Modules:
  0.0 13.1 jit_solution(7046387896089140506)
XLA Ops:
  0.6 11.8 %shard_map.41 = (f32[1,4,32,128]{3,2,1,0:T(8,128)S(1)}, f32[1,4,32,128]{3,2,1,0:T(8,128)S(1)}) custom-call(f32[1,4,32,128]{3,2,1,0:T(8,128)} %starts_ref.1, f32[4,32,128]{2,1,0:T(8,128)} %rates_ref.1), custom_call_target="tpu_custom_call" | custom-call | tf_op jit(solution)/shard_map/pallas_call | solution.py:830
  12.5 0.7 %shard_map.42 = (f32[1,4,32,128]{3,2,1,0:T(8,128)}, f32[1,4,32,128]{3,2,1,0:T(8,128)}) custom-call(f32[1,4,32,128]{3,2,1,0:T(8,128)S(1)} %get-tuple-element.4.end_ref, f32[1,4,32,128]{3,2,1,0:T(8,128)S(1)} %get-tuple-element.5.next_ref), custom_call_target="tpu_custom_call" | custom-call | tf_op jit(solution)/shard_map/pallas_call | solution.py:803
